TPU v7x, 32 devices: a whole 2x2x4 slice. The times are simulated.
32 devices in a mesh: gx: 8 (over z, x), gy: 4 (over y, core).
Axes of the slice: x: 2, y: 2, z: 4, core: 2. Of those that a mesh axis runs over, the one named last changes fastest.
Arguments:
- species: float32 [53, 32, 32, 128], P(None, 'gx', 'gy'), may hold values from -6 to 6
- diffusion: float32 [53], replicated, may hold values from 0.02 to 0.15
- class_rate: float32 [4], replicated, may hold values from 0.2 to 1
- mixing: float32 [53, 53], replicated, may hold values from -0.3 to 0.3
- inverses: float32 [4, 53, 53], replicated, may hold values from -0.01 to 0.12
- newton_counts: int32 [4], replicated, may hold values from 1 to 8, as said below
- cell_class: int32 [32, 32, 128], P('gx', 'gy'), may hold values from 0 to 3
Outputs:
- updated: float32 [53, 32, 32, 128], P(None, 'gx', 'gy')
Inputs may be any that keep to these rules, and one draw needn't show every extreme that they name: `newton_counts`: nondecreasing in the class; the last class takes 8.
All inputs are finite; a program needn't handle non-finite values.
Results may differ from a plain program's by a relative error of at most 0.0003.
Values sent between devices are 32-bit elements; how exact they have to be, the bound alone decides.
No kernel may reach another device: no remote copies, remote signals or barrier semaphores. Data moves between devices by JAX's collectives and lax.ppermute only.
A program may use at most 64 MiB of HBM per device.

v0:
```python
import functools

import jax
import jax.numpy as jnp
from jax import lax
from jax.experimental import pallas as pl
from jax.experimental.pallas import tpu as pltpu
from jax.sharding import PartitionSpec as P


F32 = jnp.float32
BF16 = jnp.bfloat16
SUB = 8
SMEM = pl.BlockSpec(memory_space=pltpu.SMEM)
VMEM = pl.BlockSpec(memory_space=pltpu.VMEM)


def up(value, step):
    return -(-value // step) * step


def swap(block, axis, first):
    count = lax.axis_size(axis)
    pairs = []
    for i in range(first, count - 1, 2):
        pairs += [(i, i + 1), (i + 1, i)]
    return lax.ppermute(block, axis, pairs)


def near_index(axis, size, inner=0):
    return jnp.where(lax.axis_index(axis) % 2 == 0, size - 1 - inner, inner)


def far_index(axis, size, inner=0):
    return jnp.where(lax.axis_index(axis) % 2 == 0, inner, size - 1 - inner)


def split(value):
    high = value.astype(BF16)
    low = (value - high.astype(F32)).astype(BF16)
    return jnp.concatenate([high, low, high], axis=0)


def widen(value, rows):
    short = rows - value.shape[0]
    if short == 0:
        return value
    return jnp.concatenate([value, jnp.zeros((short, value.shape[1]), value.dtype)], axis=0)


def put(ref, index, value, rows):
    whole = ref.shape[-2]
    if whole != rows:
        ref[(*index, slice(whole - SUB, whole), slice(None))] = jnp.zeros((SUB, ref.shape[-1]), F32)
    ref[(*index, slice(0, rows), slice(None))] = value


def newton(n, y_ref, st_ref, r1_ref, kind_ref, count, w1_ref, w2_ref, nclass):
    sp, nz = y_ref.shape[1:]
    deep = w1_ref.shape[0]
    tiles = [list(range(i, min(i + 2, n))) for i in range(0, n, 2)]

    def lanes(ref, rows):
        return jnp.concatenate([ref[r] for r in rows], axis=1)

    def tall(value):
        return jnp.concatenate([value] * (sp // SUB), axis=0)

    for low in range(nclass):
        live = nclass - low

        def body(_, carry, low=low, live=live):
            mixed = []
            for rows in tiles:
                t = widen(jnp.tanh(lanes(y_ref, rows)), deep)
                m = jnp.dot(w1_ref[...], split(t), preferred_element_type=F32)
                mixed.append(m[:sp])
            for rows, m in zip(tiles, mixed):
                y = lanes(y_ref, rows)
                g = tall(lanes(r1_ref, rows)) * y - lanes(st_ref, rows) - m
                w2 = w2_ref[: up(live * sp, 16), :]
                out = jnp.dot(w2, split(widen(g, deep)), preferred_element_type=F32)
                kind = tall(lanes(kind_ref, rows))
                step = out[(live - 1) * sp : live * sp] if low == 0 else jnp.zeros_like(y)
                for j in range(live - 1 if low == 0 else live):
                    step = jnp.where(kind == nclass - 1 - j, out[j * sp : (j + 1) * sp], step)
                y = y - step
                for i, r in enumerate(rows):
                    y_ref[r] = y[:, i * nz : (i + 1) * nz]
            return carry

        begin = 0 if low == 0 else count[low - 1]
        lax.fori_loop(begin, count[low], body, 0)


def shifted(v):
    lane = lax.broadcasted_iota(jnp.int32, v.shape, 1)
    nz = v.shape[1]
    left = jnp.where(lane == 0, 0.0, pltpu.roll(v, 1, 1))
    right = jnp.where(lane == nz - 1, 0.0, pltpu.roll(v, nz - 1, 1))
    return left + right


def lap(v, nbrs):
    total = shifted(v) - 6.0 * v
    for other in nbrs:
        total = total + other
    return total


def start_row(i, v, force, cls, rate, y_ref, st_ref, r1_ref, kind_ref, nclass):
    nz = v.shape[1]
    kind = jnp.broadcast_to(cls, (SUB, nz))
    inv = jnp.full((SUB, nz), 1.0 / rate[0], F32)
    for c in range(1, nclass):
        inv = jnp.where(kind == c, 1.0 / rate[c], inv)
    target = v + force
    y_ref[i] = target
    st_ref[i] = target * jnp.concatenate([inv] * (v.shape[0] // SUB), axis=0)
    r1_ref[i] = inv + 1.0
    kind_ref[i] = kind


def faces_kernel(nx, ny, ns, block, fa, fya, fyb):
    xa = near_index("gx", nx)
    for s in range(ns):
        fa[pl.ds(s * ny, ny), :] = block[pl.ds(s * nx * ny + xa * ny, ny), :]
    for face, y in ((fya, near_index("gy", ny)), (fyb, far_index("gy", ny))):
        for x in range(nx):
            put(face, (x,), block[pl.ds(x * ny + y, ns, stride=nx * ny), :], ns)


def inner_kernel(nx, ny, ns, nclass, rate, count, dif, block, mixing, inverses, cls,
                 s_ref, f_ref, sec, w1, w2, scale, fb,
                 y_ref, st_ref, r1_ref, kind_ref, square):
    sp, nz = s_ref.shape[2:]
    deep = square.shape[0]
    xb = far_index("gx", nx)
    for s in range(ns):
        fb[pl.ds(s * ny, ny), :] = block[pl.ds(s * nx * ny + xb * ny, ny), :]

    square[...] = jnp.zeros_like(square)

    def pack(values, rows):
        square[:ns, :ns] = values
        value = square[:rows, :]
        high = value.astype(BF16)
        back = high.astype(F32)
        return (back + pltpu.roll(back, deep, 1)).astype(BF16), (value - back).astype(BF16)[:, :deep]

    w1[:, : 2 * deep], w1[:, 2 * deep :] = pack(mixing[...], deep)
    highs, lows = [], []
    for c in reversed(range(nclass)):
        square[:ns, :ns] = inverses[c] * rate[c]
        value = square[:sp, :]
        back = value.astype(BF16).astype(F32)
        highs.append(back + pltpu.roll(back, deep, 1))
        lows.append(value - back)
    whole = w2.shape[0]
    w2[:, : 2 * deep] = widen(jnp.concatenate(highs, axis=0), whole).astype(BF16)
    w2[:, 2 * deep :] = widen(jnp.concatenate(lows, axis=0), whole).astype(BF16)[:, :deep]

    sub = lax.broadcasted_iota(jnp.int32, (SUB, nz), 0)
    for g in range(0, sp, SUB):
        value = jnp.zeros((SUB, nz), F32)
        for s in range(g, min(g + SUB, ns)):
            value = jnp.where(sub == s - g, dif[s], value)
        scale[g : g + SUB, :] = value

    for x in range(nx):
        for y in range(ny):
            put(s_ref, (x, y), block[pl.ds(x * ny + y, ns, stride=nx * ny), :], ns)
    rows = [(x, y) for x in range(1, nx - 1) for y in range(1, ny - 1)]
    for i, (x, y) in enumerate(rows):
        v = s_ref[x, y]
        force = scale[...] * lap(v, [s_ref[x - 1, y], s_ref[x + 1, y], s_ref[x, y - 1], s_ref[x, y + 1]])
        f_ref[x, y] = force
        start_row(i, v, force, cls[x, y : y + 1, :], rate, y_ref, st_ref, r1_ref, kind_ref, nclass)
    newton(len(rows), y_ref, st_ref, r1_ref, kind_ref, count, w1, w2, nclass)
    for i, (x, y) in enumerate(rows):
        sec[x, y] = y_ref[i]


def layer_rows(nx, ny, ns, near, with_edges, s_ref, halo, ya, yb):
    sp = s_ref.shape[2]
    index = near_index if near else far_index
    x0, x1 = index("gx", nx), index("gx", nx, 1)
    even_y = lax.axis_index("gy") % 2 == 0

    def edge(x, high):
        return jnp.where(even_y == high, ya[x], yb[x])

    def found(x, y, xs):
        nbrs = [get() for get in xs]
        nbrs.append(s_ref[x, y - 1] if y > 0 else edge(x, False))
        nbrs.append(s_ref[x, y + 1] if y < ny - 1 else edge(x, True))
        return x, y, s_ref[x, y], nbrs

    for y in range(ny):
        yield found(x0, y, [lambda y=y: s_ref[x1, y], lambda y=y: widen(halo[pl.ds(y, ns, stride=ny), :], sp)])
    if with_edges:
        for x in range(1, nx - 1):
            for y in (0, ny - 1):
                yield found(x, y, [lambda x=x, y=y: s_ref[x - 1, y], lambda x=x, y=y: s_ref[x + 1, y]])


def layer_kernel(nx, ny, ns, nclass, near, rate, count, s_ref, halo, ya, yb, cls, w1, w2, scale, f_in, sec_in,
                 f_ref, sec, face, *rest):
    y_ref, st_ref, r1_ref, kind_ref = rest[-4:]
    places = []
    for i, (x, y, v, nbrs) in enumerate(layer_rows(nx, ny, ns, near, near, s_ref, halo, ya, yb)):
        force = scale[...] * lap(v, nbrs)
        f_ref[x, y] = force
        start_row(i, v, force, cls[x, y : y + 1, :], rate, y_ref, st_ref, r1_ref, kind_ref, nclass)
        places.append((x, y))
    newton(len(places), y_ref, st_ref, r1_ref, kind_ref, count, w1, w2, nclass)
    for i, (x, y) in enumerate(places):
        sec[x, y] = y_ref[i]
        if i < ny:
            face[pl.ds(y, ns, stride=ny), :] = y_ref[i][:ns]
    if not near:
        fya, fyb = rest[:2]
        for out, y in ((fya, near_index("gy", ny)), (fyb, far_index("gy", ny))):
            for x in range(nx):
                out[x] = sec[x, y]


def last_kernel(nx, ny, ns, sec, f_ref, xa, xb, ya, yb, scale, out):
    sp = sec.shape[2]
    even_x = lax.axis_index("gx") % 2 == 0
    even_y = lax.axis_index("gy") % 2 == 0

    def outer(y, high):
        near = xa[pl.ds(y, ns, stride=ny), :]
        far = xb[pl.ds(y, ns, stride=ny), :]
        return widen(jnp.where(even_x == high, near, far), sp)

    for x in range(nx):
        for y in range(ny):
            v = sec[x, y]
            nbrs = [
                sec[x - 1, y] if x > 0 else outer(y, False),
                sec[x + 1, y] if x < nx - 1 else outer(y, True),
                sec[x, y - 1] if y > 0 else jnp.where(even_y == False, ya[x], yb[x]),
                sec[x, y + 1] if y < ny - 1 else jnp.where(even_y == True, ya[x], yb[x]),
            ]
            value = v + 0.5 * (scale[...] * lap(v, nbrs) - f_ref[x, y])
            out[pl.ds(x * ny + y, ns, stride=nx * ny), :] = value[:ns]


def local(species, diffusion, class_rate, mixing, inverses, newton_counts, cell_class):
    ns, nx, ny, nz = species.shape
    nclass = class_rate.shape[0]
    sp, deep = up(ns, SUB), up(ns, 16)
    block = species.reshape(ns * nx * ny, nz)
    field = jax.ShapeDtypeStruct((nx, ny, sp, nz), F32)
    xface = jax.ShapeDtypeStruct((ns * ny, nz), F32)
    yface = jax.ShapeDtypeStruct((nx, sp, nz), F32)

    def call(kernel, ins, outs, scratch=(), mib=6, work=1, alias=()):
        return pl.pallas_call(
            kernel,
            out_shape=tuple(outs),
            in_specs=[SMEM if small else VMEM for small, _ in ins],
            out_specs=(VMEM,) * len(outs),
            scratch_shapes=list(scratch),
            input_output_aliases=dict(alias),
            compiler_params=pltpu.CompilerParams(vmem_limit_bytes=mib * 2**20),
            cost_estimate=pl.CostEstimate(flops=work, bytes_accessed=1, transcendentals=0),
        )(*[value for _, value in ins])

    def scratch(n):
        return [
            pltpu.VMEM((n, sp, nz), F32),
            pltpu.VMEM((n, sp, nz), F32),
            pltpu.VMEM((n, SUB, nz), F32),
            pltpu.VMEM((n, SUB, nz), jnp.int32),
        ]

    big = lambda *values: [(False, v) for v in values]
    small = lambda *values: [(True, v) for v in values]
    us = 10**9

    fa, fya, fyb = call(functools.partial(faces_kernel, nx, ny, ns), big(block), [xface, yface, yface], work=us // 2)
    ha = swap(fa, "gx", 0)
    hya = swap(fya, "gy", 0)
    hyb = swap(fyb, "gy", 1)

    s_ref, force, sec, w1, w2, scale, fb = call(
        functools.partial(inner_kernel, nx, ny, ns, nclass),
        small(class_rate, newton_counts, diffusion) + big(block, mixing, inverses, cell_class),
        [
            field,
            field,
            field,
            jax.ShapeDtypeStruct((deep, 3 * deep), BF16),
            jax.ShapeDtypeStruct((up(nclass * sp, 16), 3 * deep), BF16),
            jax.ShapeDtypeStruct((sp, nz), F32),
            xface,
        ],
        scratch((nx - 2) * (ny - 2)) + [pltpu.VMEM((deep, 2 * deep), F32)],
        mib=10,
        work=4 * us,
    )
    hb = swap(fb, "gx", 1)

    def layer(near, halo, force, sec):
        n = ny + (2 * (nx - 2) if near else 0)
        ins = small(class_rate, newton_counts) + big(s_ref, halo, hya, hyb, cell_class, w1, w2, scale, force, sec)
        outs = [field, field, xface] + ([] if near else [yface, yface])
        kernel = functools.partial(layer_kernel, nx, ny, ns, nclass, near)
        return call(kernel, ins, outs, scratch(n), mib=10, work=4 * us, alias=((10, 0), (11, 1)))

    force, sec, fa = layer(True, ha, force, sec)
    ha = swap(fa, "gx", 0)
    force, sec, fb, fya, fyb = layer(False, hb, force, sec)
    hb = swap(fb, "gx", 1)
    hya = swap(fya, "gy", 0)
    hyb = swap(fyb, "gy", 1)
    (out,) = call(
        functools.partial(last_kernel, nx, ny, ns),
        big(sec, force, ha, hb, hya, hyb, scale),
        [jax.ShapeDtypeStruct(block.shape, F32)],
        work=2 * us,
    )
    return out.reshape(species.shape)


def solution(mesh):
    in_specs = (P(None, "gx", "gy", None), P(), P(), P(), P(), P(), P("gx", "gy", None))
    out_specs = P(None, "gx", "gy", None)


    return jax.shard_map(local, mesh=mesh, in_specs=in_specs, out_specs=out_specs, check_vma=False)
```

profile of v0, /device:TPU:17, one launch (start us, length us, event | category | flops | bytes accessed | tf_op | source)
XLA Modules:
  0.0 40.2 jit_solution(14289235773489304931)
XLA Ops:
  0.0 0.0 copy-start
  0.0 1.2 %copy-done = f32[53,4,8,128]{3,2,1,0:T(8,128)S(1)} copy-done((f32[53,4,8,128]{3,2,1,0:T(8,128)S(1)}, f32[53,4,8,128]{3,2,1,0:T(8,128)}, u32[]{:S(2)}) %copy-start) | copy-done | bytes 868376
  1.2 0.0 copy-start.7
  1.2 0.0 copy-start.1
  1.2 0.2 shard_map.74
  1.3 0.7 %collective-permute-start.1 = (f32[4,56,128]{2,1,0:T(8,128)S(1)}, f32[4,56,128]{2,1,0:T(8,128)S(1)}, u32[]{:S(2)}, u32[]{:S(2)}) collective-permute-start(f32[4,56,128]{2,1,0:T(8,128)S(1)} %get-tuple-element.25), channel_id=1, source_target_pairs={{0,1},{1,0},{2,3},{3,2},{4,5},{5,4},{6,7},{7,6},{8,9},{9,8},{10,11... | collective-permute-start | bytes 344072 | tf_op jit(solution)/shard_map/ppermute | solution.py:27
  2.1 3.2 %collective-permute-start.2 = (f32[4,56,128]{2,1,0:T(8,128)S(1)}, f32[4,56,128]{2,1,0:T(8,128)S(1)}, u32[]{:S(2)}, u32[]{:S(2)}) collective-permute-start(f32[4,56,128]{2,1,0:T(8,128)S(1)} %get-tuple-element.26), channel_id=1, source_target_pairs={{1,2},{2,1},{5,6},{6,5},{9,10},{10,9},{13,14},{14,13},{17,18},{18,... | collective-permute-start | bytes 344072 | tf_op jit(solution)/shard_map/ppermute | solution.py:27
  5.3 0.0 copy-start.2
  5.3 0.0 copy-start.3
  5.3 0.0 copy-start.4
  5.3 0.0 copy-start.5
  5.3 0.0 copy-start.6
  5.3 1.3 %collective-permute-start.3 = (f32[424,128]{1,0:T(8,128)S(1)}, f32[424,128]{1,0:T(8,128)S(1)}, u32[]{:S(2)}, u32[]{:S(2)}) collective-permute-start(f32[424,128]{1,0:T(8,128)S(1)} %get-tuple-element.30), channel_id=1, source_target_pairs={{0,4},{4,0},{8,12},{12,8},{16,20},{20,16},{24,28},{28,24},{1,5},{5... | collective-permute-start | bytes 651272 | tf_op jit(solution)/shard_map/ppermute | solution.py:27
  6.6 0.0 copy-done.7
  6.6 0.0 copy-done.1
  6.6 0.0 copy-done.2
  6.6 0.0 copy-done.3
  6.6 0.0 copy-done.4
  6.7 0.0 copy-done.5
  6.7 0.0 copy-done.6
  6.7 4.8 %shard_map.73 = (f32[4,8,56,128]{3,2,1,0:T(8,128)S(1)}, f32[4,8,56,128]{3,2,1,0:T(8,128)S(1)}, f32[4,8,56,128]{3,2,1,0:T(8,128)S(1)}, bf16[64,192]{1,0:T(8,128)(...) custom-call(f32[4]{0:T(128)S(1)} %copy-done.5, s32[4]{0:T(128)S(1)} %copy-done.6, ...), custom_call_target="tpu_custom_call" | custom-call | flops 4000000000 | bytes 1 | tf_op jit(solution)/shard_map/pallas_call | solution.py:261
  11.5 2.4 %collective-permute-start = (f32[424,128]{1,0:T(8,128)S(1)}, f32[424,128]{1,0:T(8,128)S(1)}, u32[]{:S(2)}, u32[]{:S(2)}) collective-permute-start(f32[424,128]{1,0:T(8,128)S(1)} %get-tuple-element.24), channel_id=1, source_target_pairs={{4,8},{8,4},{12,16},{16,12},{20,24},{24,20},{5,9},{9,5},{13,17},{1... | collective-permute-start | bytes 651272 | tf_op jit(solution)/shard_map/ppermute | solution.py:27
  13.9 0.0 collective-permute-done.1.ya
  13.9 0.0 collective-permute-done.2.yb
  13.9 0.0 collective-permute-done.3.halo
  13.9 4.4 %shard_map.75 = (f32[4,8,56,128]{3,2,1,0:T(8,128)S(1)}, f32[4,8,56,128]{3,2,1,0:T(8,128)S(1)}, f32[424,128]{1,0:T(8,128)S(1)}) custom-call(f32[4]{0:T(128)S(1)} %copy-done.5, s32[4]{0:T(128)S(1)} %copy-done.6, f32[4,8,56,128]{3,2,1,0:T(8,128)S(1)} %get-tuple-element.23.s_ref, ...), custom_call_target="tpu_custom_call", output_to_operand_aliasing={{0}: (10, {}), {1}: (11, {})} | custom-call | flops 4000000000 | bytes 1 | tf_op jit(solution)/shard_map/pallas_call | solution.py:261
  18.3 1.4 %collective-permute-done.halo = f32[424,128]{1,0:T(8,128)S(1)} collective-permute-done((f32[424,128]{1,0:T(8,128)S(1)}, f32[424,128]{1,0:T(8,128)S(1)}, u32[]{:S(2)}, u32[]{:S(2)}) %collective-permute-start) | collective-permute-done | bytes 217120 | tf_op jit(solution)/shard_map/ppermute | solution.py:27
  19.7 3.9 %shard_map.76 = (f32[4,8,56,128]{3,2,1,0:T(8,128)S(1)}, f32[4,8,56,128]{3,2,1,0:T(8,128)S(1)}, f32[424,128]{1,0:T(8,128)S(1)}, f32[4,56,128]{2,1,0:T(8,128)S(1)}, f32[4,56,128]{2,1,0:T(8,128)S(1)}) custom-call(f32[4]{0:T(128)S(1)} %copy-done.5, s32[4]{0:T(128)S(1)} %copy-done.6, ...), custom_call_target="tpu_custom_call", output_to_operand_aliasing={{0}: (10, {}), {1}: (11, {})} | custom-call | flops 4000000000 | bytes 1 | tf_op jit(solution)/shard_map/pallas_call | solution.py:261
  23.7 2.4 %collective-permute-start.5 = (f32[424,128]{1,0:T(8,128)S(1)}, f32[424,128]{1,0:T(8,128)S(1)}, u32[]{:S(2)}, u32[]{:S(2)}) collective-permute-start(f32[424,128]{1,0:T(8,128)S(1)} %get-tuple-element.38), channel_id=1, source_target_pairs={{4,8},{8,4},{12,16},{16,12},{20,24},{24,20},{5,9},{9,5},{13,17},{1... | collective-permute-start | bytes 651272 | tf_op jit(solution)/shard_map/ppermute | solution.py:27
  26.1 2.1 %collective-permute-start.4 = (f32[424,128]{1,0:T(8,128)S(1)}, f32[424,128]{1,0:T(8,128)S(1)}, u32[]{:S(2)}, u32[]{:S(2)}) collective-permute-start(f32[424,128]{1,0:T(8,128)S(1)} %get-tuple-element.37), channel_id=1, source_target_pairs={{0,4},{4,0},{8,12},{12,8},{16,20},{20,16},{24,28},{28,24},{1,5},{5... | collective-permute-start | bytes 651272 | tf_op jit(solution)/shard_map/ppermute | solution.py:27
  28.1 0.0 collective-permute-start.6
  28.1 3.7 %collective-permute-start.7 = (f32[4,56,128]{2,1,0:T(8,128)S(1)}, f32[4,56,128]{2,1,0:T(8,128)S(1)}, u32[]{:S(2)}, u32[]{:S(2)}) collective-permute-start(f32[4,56,128]{2,1,0:T(8,128)S(1)} %get-tuple-element.40), channel_id=1, source_target_pairs={{1,2},{2,1},{5,6},{6,5},{9,10},{10,9},{13,14},{14,13},{17,18},{18,... | collective-permute-start | bytes 344072 | tf_op jit(solution)/shard_map/ppermute | solution.py:27
  31.8 0.0 collective-permute-done.6.ya
  31.8 2.7 %collective-permute-done.7.yb = f32[4,56,128]{2,1,0:T(8,128)S(1)} collective-permute-done((f32[4,56,128]{2,1,0:T(8,128)S(1)}, f32[4,56,128]{2,1,0:T(8,128)S(1)}, u32[]{:S(2)}, u32[]{:S(2)}) %collective-permute-start.7) | collective-permute-done | bytes 114720 | tf_op jit(solution)/shard_map/ppermute | solution.py:27
  34.6 0.0 collective-permute-done.5.xb
  34.6 3.4 %collective-permute-done.4.xa = f32[424,128]{1,0:T(8,128)S(1)} collective-permute-done((f32[424,128]{1,0:T(8,128)S(1)}, f32[424,128]{1,0:T(8,128)S(1)}, u32[]{:S(2)}, u32[]{:S(2)}) %collective-permute-start.4) | collective-permute-done | bytes 217120 | tf_op jit(solution)/shard_map/ppermute | solution.py:27
  38.0 2.2 %shard_map.77 = f32[1696,128]{1,0:T(8,128)} custom-call(f32[4,8,56,128]{3,2,1,0:T(8,128)S(1)} %get-tuple-element.35.sec, f32[4,8,56,128]{3,2,1,0:T(8,128)S(1)} %get-tuple-element.36.f_ref, f32[424,128]{1,0:T(8,128)S(1)} %collective-permute-done.4.xa, f32[424,128]{1,0:T(8,128)S(1)} %collective-permute-done.5.xb, f32[4,56,128]{2,1,0:T(8,128)S(1)} %collective-permute-done.6.ya, ...), custom_call_target="tpu_custom_call" | custom-call | flops 2000000000 | bytes 1 | tf_op jit(solution)/shard_map/pallas_call | solution.py:261
  (1 shorter events, 0.0 us)
Async XLA Ops:
  0.0 1.2 %copy-start = (f32[53,4,8,128]{3,2,1,0:T(8,128)S(1)}, f32[53,4,8,128]{3,2,1,0:T(8,128)}, u32[]{:S(2)}) copy-start(f32[53,4,8,128]{3,2,1,0:T(8,128)} %param.7) | copy-start | bytes 2605060
  1.2 5.4 %copy-start.7 = (f32[4,53,53]{2,0,1:T(4,128)S(1)}, f32[4,53,53]{2,0,1:T(4,128)}, u32[]{:S(2)}) copy-start(f32[4,53,53]{2,0,1:T(4,128)} %param.11) | copy-start | bytes 134836
  1.2 5.5 %copy-start.1 = (f32[53,4,8,128]{3,2,1,0:T(8,128)S(1)}, f32[53,4,8,128]{3,2,1,0:T(8,128)}, u32[]{:S(2)}) copy-start(f32[53,4,8,128]{3,2,1,0:T(8,128)} %param.7) | copy-start | bytes 2605060
  1.3 12.5 %collective-permute-start.1 = (f32[4,56,128]{2,1,0:T(8,128)S(1)}, f32[4,56,128]{2,1,0:T(8,128)S(1)}, u32[]{:S(2)}, u32[]{:S(2)}) collective-permute-start(f32[4,56,128]{2,1,0:T(8,128)S(1)} %get-tuple-element.25), channel_id=1, source_target_pairs={{0,1},{1,0},{2,3},{3,2},{4,5},{5,4},{6,7},{7,6},{8,9},{9,8},{10,11... | collective-permute-start | bytes 344072 | tf_op jit(solution)/shard_map/ppermute | solution.py:27
  2.1 11.8 %collective-permute-start.2 = (f32[4,56,128]{2,1,0:T(8,128)S(1)}, f32[4,56,128]{2,1,0:T(8,128)S(1)}, u32[]{:S(2)}, u32[]{:S(2)}) collective-permute-start(f32[4,56,128]{2,1,0:T(8,128)S(1)} %get-tuple-element.26), channel_id=1, source_target_pairs={{1,2},{2,1},{5,6},{6,5},{9,10},{10,9},{13,14},{14,13},{17,18},{18,... | collective-permute-start | bytes 344072 | tf_op jit(solution)/shard_map/ppermute | solution.py:27
  5.3 1.4 %copy-start.2 = (f32[53,53]{1,0:T(8,128)S(1)}, f32[53,53]{1,0:T(8,128)}, u32[]{:S(2)}) copy-start(f32[53,53]{1,0:T(8,128)} %mixing.1) | copy-start | bytes 33712
  5.3 1.4 %copy-start.3 = (s32[4,8,128]{2,1,0:T(8,128)S(1)}, s32[4,8,128]{2,1,0:T(8,128)}, u32[]{:S(2)}) copy-start(s32[4,8,128]{2,1,0:T(8,128)} %cls.5) | copy-start | bytes 49156
  5.3 1.4 %copy-start.4 = (f32[53]{0:T(128)S(1)}, f32[53]{0:T(128)}, u32[]{:S(2)}) copy-start(f32[53]{0:T(128)} %dif.1) | copy-start | bytes 640
  5.3 1.4 %copy-start.5 = (f32[4]{0:T(128)S(1)}, f32[4]{0:T(128)}, u32[]{:S(2)}) copy-start(f32[4]{0:T(128)} %rate.5) | copy-start | bytes 52
  5.3 1.4 %copy-start.6 = (s32[4]{0:T(128)S(1)}, s32[4]{0:T(128)}, u32[]{:S(2)}) copy-start(s32[4]{0:T(128)} %count.5) | copy-start | bytes 52
  5.3 8.6 %collective-permute-start.3 = (f32[424,128]{1,0:T(8,128)S(1)}, f32[424,128]{1,0:T(8,128)S(1)}, u32[]{:S(2)}, u32[]{:S(2)}) collective-permute-start(f32[424,128]{1,0:T(8,128)S(1)} %get-tuple-element.30), channel_id=1, source_target_pairs={{0,4},{4,0},{8,12},{12,8},{16,20},{20,16},{24,28},{28,24},{1,5},{5... | collective-permute-start | bytes 651272 | tf_op jit(solution)/shard_map/ppermute | solution.py:27
  11.5 8.2 %collective-permute-start = (f32[424,128]{1,0:T(8,128)S(1)}, f32[424,128]{1,0:T(8,128)S(1)}, u32[]{:S(2)}, u32[]{:S(2)}) collective-permute-start(f32[424,128]{1,0:T(8,128)S(1)} %get-tuple-element.24), channel_id=1, source_target_pairs={{4,8},{8,4},{12,16},{16,12},{20,24},{24,20},{5,9},{9,5},{13,17},{1... | collective-permute-start | bytes 651272 | tf_op jit(solution)/shard_map/ppermute | solution.py:27
  23.7 10.9 %collective-permute-start.5 = (f32[424,128]{1,0:T(8,128)S(1)}, f32[424,128]{1,0:T(8,128)S(1)}, u32[]{:S(2)}, u32[]{:S(2)}) collective-permute-start(f32[424,128]{1,0:T(8,128)S(1)} %get-tuple-element.38), channel_id=1, source_target_pairs={{4,8},{8,4},{12,16},{16,12},{20,24},{24,20},{5,9},{9,5},{13,17},{1... | collective-permute-start | bytes 651272 | tf_op jit(solution)/shard_map/ppermute | solution.py:27
  26.1 11.9 %collective-permute-start.4 = (f32[424,128]{1,0:T(8,128)S(1)}, f32[424,128]{1,0:T(8,128)S(1)}, u32[]{:S(2)}, u32[]{:S(2)}) collective-permute-start(f32[424,128]{1,0:T(8,128)S(1)} %get-tuple-element.37), channel_id=1, source_target_pairs={{0,4},{4,0},{8,12},{12,8},{16,20},{20,16},{24,28},{28,24},{1,5},{5... | collective-permute-start | bytes 651272 | tf_op jit(solution)/shard_map/ppermute | solution.py:27
  28.1 3.7 %collective-permute-start.6 = (f32[4,56,128]{2,1,0:T(8,128)S(1)}, f32[4,56,128]{2,1,0:T(8,128)S(1)}, u32[]{:S(2)}, u32[]{:S(2)}) collective-permute-start(f32[4,56,128]{2,1,0:T(8,128)S(1)} %get-tuple-element.39), channel_id=1, source_target_pairs={{0,1},{1,0},{2,3},{3,2},{4,5},{5,4},{6,7},{7,6},{8,9},{9,8},{10,11... | collective-permute-start | bytes 344072 | tf_op jit(solution)/shard_map/ppermute | solution.py:27
  28.1 6.4 %collective-permute-start.7 = (f32[4,56,128]{2,1,0:T(8,128)S(1)}, f32[4,56,128]{2,1,0:T(8,128)S(1)}, u32[]{:S(2)}, u32[]{:S(2)}) collective-permute-start(f32[4,56,128]{2,1,0:T(8,128)S(1)} %get-tuple-element.40), channel_id=1, source_target_pairs={{1,2},{2,1},{5,6},{6,5},{9,10},{10,9},{13,14},{14,13},{17,18},{18,... | collective-permute-start | bytes 344072 | tf_op jit(solution)/shard_map/ppermute | solution.py:27
where the time goes:
time: 40.5 us; the launch traced here: 40.2 us
  starting transfers between devices  15.7 us (39%)
  Pallas kernels  15.5 us (38%)
  waiting for transfers between devices  7.61 us (19%)
  local copies, waits for them, and re-layouts  1.21 us (3%)
    ppermute x8, starting transfers between devices, swap(): return lax.ppermute(block, axis, pairs)  15.7 us
    pallas_call x5, Pallas kernels, call(): pl.pallas_call(kernel, out_shape=tuple(outs), in_specs=[SMEM if small els...  15.5 us
    ppermute x8, waiting for transfers between devices, swap(): return lax.ppermute(block, axis, pairs)  7.61 us
    unnamed x17, local copies, waits for them, and re-layouts  1.21 us
  transfers between devices with their start and end apart: 8, of which 3 were waited for; matrix products, arithmetic and copies ran while one was open for 0% of the time, Pallas kernels for 23%

commit v1 on v0

v1 whole, which is shorter than its diff:
```python
import functools

import jax
import jax.numpy as jnp
from jax import lax
from jax.experimental import pallas as pl
from jax.experimental.pallas import tpu as pltpu
from jax.sharding import PartitionSpec as P


F32 = jnp.float32
BF16 = jnp.bfloat16
SUB = 8
SMEM = pl.BlockSpec(memory_space=pltpu.SMEM)
VMEM = pl.BlockSpec(memory_space=pltpu.VMEM)


def up(value, step):
    return -(-value // step) * step


def swap(block, axis, first):
    count = lax.axis_size(axis)
    pairs = []
    for i in range(first, count - 1, 2):
        pairs += [(i, i + 1), (i + 1, i)]
    return lax.ppermute(block, axis, pairs)


def near_index(axis, size, inner=0):
    return jnp.where(lax.axis_index(axis) % 2 == 0, size - 1 - inner, inner)


def far_index(axis, size, inner=0):
    return jnp.where(lax.axis_index(axis) % 2 == 0, inner, size - 1 - inner)


def split(value):
    high = value.astype(BF16)
    low = (value - high.astype(F32)).astype(BF16)
    return jnp.concatenate([high, low, high], axis=0)


def widen(value, rows):
    short = rows - value.shape[0]
    if short == 0:
        return value
    return jnp.concatenate([value, jnp.zeros((short, value.shape[1]), value.dtype)], axis=0)


def put(ref, index, value, rows):
    whole = ref.shape[-2]
    if whole != rows:
        ref[(*index, slice(whole - SUB, whole), slice(None))] = jnp.zeros((SUB, ref.shape[-1]), F32)
    ref[(*index, slice(0, rows), slice(None))] = value


def newton(n, y_ref, st_ref, r1_ref, kind_ref, count, w1_ref, w2_ref, nclass):
    sp, nz = y_ref.shape[1:]
    deep = w1_ref.shape[0]
    tiles = [list(range(i, min(i + 2, n))) for i in range(0, n, 2)]

    def lanes(ref, rows):
        return jnp.concatenate([ref[r] for r in rows], axis=1)

    def tall(value):
        return jnp.concatenate([value] * (sp // SUB), axis=0)

    for low in range(nclass):
        live = nclass - low

        def body(_, carry, low=low, live=live):
            mixed = []
            for rows in tiles:
                t = widen(jnp.tanh(lanes(y_ref, rows)), deep)
                m = jnp.dot(w1_ref[...], split(t), preferred_element_type=F32)
                mixed.append(m[:sp])
            for rows, m in zip(tiles, mixed):
                y = lanes(y_ref, rows)
                g = tall(lanes(r1_ref, rows)) * y - lanes(st_ref, rows) - m
                w2 = w2_ref[: up(live * sp, 16), :]
                out = jnp.dot(w2, split(widen(g, deep)), preferred_element_type=F32)
                kind = tall(lanes(kind_ref, rows))
                step = out[(live - 1) * sp : live * sp] if low == 0 else jnp.zeros_like(y)
                for j in range(live - 1 if low == 0 else live):
                    step = jnp.where(kind == nclass - 1 - j, out[j * sp : (j + 1) * sp], step)
                y = y - step
                for i, r in enumerate(rows):
                    y_ref[r] = y[:, i * nz : (i + 1) * nz]
            return carry

        begin = 0 if low == 0 else count[low - 1]
        lax.fori_loop(begin, count[low], body, 0)


def shifted(v):
    lane = lax.broadcasted_iota(jnp.int32, v.shape, 1)
    nz = v.shape[1]
    left = jnp.where(lane == 0, 0.0, pltpu.roll(v, 1, 1))
    right = jnp.where(lane == nz - 1, 0.0, pltpu.roll(v, nz - 1, 1))
    return left + right


def lap(v, nbrs):
    total = shifted(v) - 6.0 * v
    for other in nbrs:
        total = total + other
    return total


def start_row(i, target, cls, rate, y_ref, st_ref, r1_ref, kind_ref, nclass):
    sp, nz = target.shape
    kind = jnp.broadcast_to(cls, (SUB, nz))
    inv = jnp.full((SUB, nz), 1.0 / rate[0], F32)
    for c in range(1, nclass):
        inv = jnp.where(kind == c, 1.0 / rate[c], inv)
    y_ref[i] = target
    st_ref[i] = target * jnp.concatenate([inv] * (sp // SUB), axis=0)
    r1_ref[i] = inv + 1.0
    kind_ref[i] = kind


def faces_kernel(nx, ny, ns, block, fa, fya, fyb):
    xa = near_index("gx", nx)
    for s in range(ns):
        fa[pl.ds(s * ny, ny), :] = block[pl.ds(s * nx * ny + xa * ny, ny), :]
    for face, y in ((fya, near_index("gy", ny)), (fyb, far_index("gy", ny))):
        for x in range(nx):
            put(face, (x,), block[pl.ds(x * ny + y, ns, stride=nx * ny), :], ns)


def make_scale(scale, dif, ns):
    sp, nz = scale.shape
    sub = lax.broadcasted_iota(jnp.int32, (SUB, nz), 0)
    for g in range(0, sp, SUB):
        value = jnp.zeros((SUB, nz), F32)
        for s in range(g, min(g + SUB, ns)):
            value = jnp.where(sub == s - g, dif[s], value)
        scale[g : g + SUB, :] = value


def make_weights(w1, w2, square, mixing, inverses, rate, ns, sp, nclass):
    deep = square.shape[0]
    square[...] = jnp.zeros_like(square)
    square[:ns, :ns] = mixing[...]
    value = square[...]
    back = value.astype(BF16).astype(F32)
    w1[:, : 2 * deep] = (back + pltpu.roll(back, deep, 1)).astype(BF16)
    w1[:, 2 * deep :] = (value - back).astype(BF16)[:, :deep]
    highs, lows = [], []
    for c in reversed(range(nclass)):
        square[:ns, :ns] = inverses[c] * rate[c]
        value = square[:sp, :]
        back = value.astype(BF16).astype(F32)
        highs.append(back + pltpu.roll(back, deep, 1))
        lows.append(value - back)
    whole = w2.shape[0]
    w2[:, : 2 * deep] = widen(jnp.concatenate(highs, axis=0), whole).astype(BF16)
    w2[:, 2 * deep :] = widen(jnp.concatenate(lows, axis=0), whole).astype(BF16)[:, :deep]


def edge_rows(ya, yb):
    even_y = lax.axis_index("gy") % 2 == 0
    return lambda x, high: jnp.where(even_y == high, ya[x], yb[x])


def send_kernel(nx, ny, ns, dif, block, ya, yb, cls, s_ref, scale, message):
    make_scale(scale, dif, ns)
    far, inner = far_index("gx", nx), far_index("gx", nx, 1)
    edge = edge_rows(ya, yb)
    for x in range(nx):
        for y in range(ny):
            put(s_ref, (x, y), block[pl.ds(x * ny + y, ns, stride=nx * ny), :], ns)
    for s in range(ns):
        message[pl.ds(s * ny, ny), :] = block[pl.ds(s * nx * ny + far * ny, ny), :]
    for y in range(ny):
        v = s_ref[far, y]
        low = s_ref[far, y - 1] if y > 0 else edge(far, False)
        high = s_ref[far, y + 1] if y < ny - 1 else edge(far, True)
        part = v + scale[...] * lap(v, [s_ref[inner, y], low, high])
        message[pl.ds(ns * ny + y, ns, stride=ny), :] = part[:ns]
    message[pl.ds(2 * ns * ny, ny), :] = cls[far].astype(F32)


def near_kernel(nx, ny, ns, nclass, rate, count, s_ref, halo, ya, yb, mixing, inverses, cls, scale,
                f_ref, sec, face, w1, w2, y_ref, st_ref, r1_ref, kind_ref, square):
    sp = s_ref.shape[2]
    make_weights(w1, w2, square, mixing, inverses, rate, ns, sp, nclass)
    edge = edge_rows(ya, yb)
    near, inner = near_index("gx", nx), near_index("gx", nx, 1)
    places = [(near, y) for y in range(ny)] + [(x, y) for x in range(1, nx - 1) for y in range(ny)]
    for i, (x, y) in enumerate(places):
        if i < ny:
            nbrs = [s_ref[inner, y], widen(halo[pl.ds(y, ns, stride=ny), :], sp)]
        else:
            nbrs = [s_ref[x - 1, y], s_ref[x + 1, y]]
        nbrs.append(s_ref[x, y - 1] if y > 0 else edge(x, False))
        nbrs.append(s_ref[x, y + 1] if y < ny - 1 else edge(x, True))
        v = s_ref[x, y]
        force = scale[...] * lap(v, nbrs)
        f_ref[x, y] = force
        start_row(i, v + force, cls[x, y : y + 1, :], rate, y_ref, st_ref, r1_ref, kind_ref, nclass)
    newton(len(places), y_ref, st_ref, r1_ref, kind_ref, count, w1, w2, nclass)
    for i, (x, y) in enumerate(places):
        sec[x, y] = y_ref[i]
        if i < ny:
            face[pl.ds(y, ns, stride=ny), :] = y_ref[i][:ns]


def far_kernel(nx, ny, ns, nclass, rate, count, s_ref, message, ya, yb, cls, scale, w1, w2, f_in, sec_in,
               f_ref, sec, beyond, fya, fyb, y_ref, st_ref, r1_ref, kind_ref):
    sp = s_ref.shape[2]
    edge = edge_rows(ya, yb)
    far, inner = far_index("gx", nx), far_index("gx", nx, 1)
    me, last = lax.axis_index("gx"), lax.axis_size("gx") - 1
    has = jnp.where(me % 2 == 0, me > 0, me < last)
    for y in range(ny):
        v = s_ref[far, y]
        nbrs = [
            s_ref[inner, y],
            widen(message[pl.ds(y, ns, stride=ny), :], sp),
            s_ref[far, y - 1] if y > 0 else edge(far, False),
            s_ref[far, y + 1] if y < ny - 1 else edge(far, True),
        ]
        force = scale[...] * lap(v, nbrs)
        f_ref[far, y] = force
        start_row(y, v + force, cls[far, y : y + 1, :], rate, y_ref, st_ref, r1_ref, kind_ref, nclass)
        target = widen(message[pl.ds(ns * ny + y, ns, stride=ny), :], sp) + scale[...] * v
        kind = message[pl.ds(2 * ns * ny + y, 1), :].astype(jnp.int32)
        start_row(ny + y, target, kind, rate, y_ref, st_ref, r1_ref, kind_ref, nclass)
    newton(2 * ny, y_ref, st_ref, r1_ref, kind_ref, count, w1, w2, nclass)
    for y in range(ny):
        sec[far, y] = y_ref[y]
        beyond[y] = jnp.where(has, y_ref[ny + y], 0.0)
    for out, y in ((fya, near_index("gy", ny)), (fyb, far_index("gy", ny))):
        for x in range(nx):
            out[x] = sec[x, y]


def last_kernel(nx, ny, ns, sec, f_ref, xa, beyond, ya, yb, scale, out):
    sp = sec.shape[2]
    even_x = lax.axis_index("gx") % 2 == 0
    edge = edge_rows(ya, yb)

    def outer(y, high):
        near = widen(xa[pl.ds(y, ns, stride=ny), :], sp)
        return jnp.where(even_x == high, near, beyond[y])

    for x in range(nx):
        for y in range(ny):
            v = sec[x, y]
            nbrs = [
                sec[x - 1, y] if x > 0 else outer(y, False),
                sec[x + 1, y] if x < nx - 1 else outer(y, True),
                sec[x, y - 1] if y > 0 else edge(x, False),
                sec[x, y + 1] if y < ny - 1 else edge(x, True),
            ]
            value = v + 0.5 * (scale[...] * lap(v, nbrs) - f_ref[x, y])
            out[pl.ds(x * ny + y, ns, stride=nx * ny), :] = value[:ns]


def local(species, diffusion, class_rate, mixing, inverses, newton_counts, cell_class):
    ns, nx, ny, nz = species.shape
    nclass = class_rate.shape[0]
    sp, deep = up(ns, SUB), up(ns, 16)
    block = species.reshape(ns * nx * ny, nz)

    def shape(*dims, dtype=F32):
        return jax.ShapeDtypeStruct(dims, dtype)

    field = shape(nx, ny, sp, nz)
    xface = shape(ns * ny, nz)
    yface = shape(nx, sp, nz)

    def call(kernel, small, big, outs, scratch=(), mib=6, work=1, alias=()):
        return pl.pallas_call(
            kernel,
            out_shape=tuple(outs),
            in_specs=[SMEM] * len(small) + [VMEM] * len(big),
            out_specs=(VMEM,) * len(outs),
            scratch_shapes=list(scratch),
            input_output_aliases=dict(alias),
            compiler_params=pltpu.CompilerParams(vmem_limit_bytes=mib * 2**20),
            cost_estimate=pl.CostEstimate(flops=work, bytes_accessed=1, transcendentals=0),
        )(*small, *big)

    def scratch(n):
        return [
            pltpu.VMEM((n, sp, nz), F32),
            pltpu.VMEM((n, sp, nz), F32),
            pltpu.VMEM((n, SUB, nz), F32),
            pltpu.VMEM((n, SUB, nz), jnp.int32),
        ]

    us = 10**9
    fa, fya, fyb = call(functools.partial(faces_kernel, nx, ny, ns), [], [block], [xface, yface, yface])
    ha = swap(fa, "gx", 0)
    hya = swap(fya, "gy", 0)
    hyb = swap(fyb, "gy", 1)
    s_ref, scale, message = call(
        functools.partial(send_kernel, nx, ny, ns),
        [diffusion],
        [block, hya, hyb, cell_class],
        [field, shape(sp, nz), shape(2 * ns * ny + ny, nz)],
        work=us,
    )
    message = swap(message, "gx", 1)
    force, sec, fa, w1, w2 = call(
        functools.partial(near_kernel, nx, ny, ns, nclass),
        [class_rate, newton_counts],
        [s_ref, ha, hya, hyb, mixing, inverses, cell_class, scale],
        [field, field, xface, shape(deep, 3 * deep, dtype=BF16), shape(up(nclass * sp, 16), 3 * deep, dtype=BF16)],
        scratch((nx - 1) * ny) + [pltpu.VMEM((deep, 2 * deep), F32)],
        mib=14,
        work=6 * us,
    )
    ha = swap(fa, "gx", 0)
    force, sec, beyond, fya, fyb = call(
        functools.partial(far_kernel, nx, ny, ns, nclass),
        [class_rate, newton_counts],
        [s_ref, message, hya, hyb, cell_class, scale, w1, w2, force, sec],
        [field, field, shape(ny, sp, nz), yface, yface],
        scratch(2 * ny),
        mib=12,
        work=4 * us,
        alias=((10, 0), (11, 1)),
    )
    hya = swap(fya, "gy", 0)
    hyb = swap(fyb, "gy", 1)
    (out,) = call(
        functools.partial(last_kernel, nx, ny, ns),
        [],
        [sec, force, ha, beyond, hya, hyb, scale],
        [shape(*block.shape)],
        work=2 * us,
    )
    return out.reshape(species.shape)


def solution(mesh):
    in_specs = (P(None, "gx", "gy", None), P(), P(), P(), P(), P(), P("gx", "gy", None))
    out_specs = P(None, "gx", "gy", None)


    return jax.shard_map(local, mesh=mesh, in_specs=in_specs, out_specs=out_specs, check_vma=False)
```

time: 40.5 us -> 36.6 us (0.904)
  the two profiles are of different devices: /device:TPU:17 before, /device:TPU:1 now
where the time goes in v1:
time: 36.6 us; the launch traced here: 36.3 us
  Pallas kernels  14.5 us (40%)
  starting transfers between devices  14.3 us (39%)
  waiting for transfers between devices  4.63 us (13%)
  local copies, waits for them, and re-layouts  2.73 us (7%)
    pallas_call x5, Pallas kernels, call(): pl.pallas_call(kernel, out_shape=tuple(outs), in_specs=[SMEM] * len(small...  14.5 us
    ppermute x7, starting transfers between devices, swap(): return lax.ppermute(block, axis, pairs)  14.3 us
    ppermute x7, waiting for transfers between devices, swap(): return lax.ppermute(block, axis, pairs)  4.63 us
    unnamed x15, local copies, waits for them, and re-layouts  2.73 us
  transfers between devices with their start and end apart: 7, of which 2 were waited for; matrix products, arithmetic and copies ran while one was open for 3% of the time, Pallas kernels for 33%

profile of v1, /device:TPU:1, one launch (start us, length us, event | category | flops | bytes accessed | tf_op | source)
XLA Modules:
  0.0 36.3 jit_solution(9790018838601900343)
XLA Ops:
  0.0 0.0 copy-start
  0.0 1.2 %copy-done = f32[53,4,8,128]{3,2,1,0:T(8,128)S(1)} copy-done((f32[53,4,8,128]{3,2,1,0:T(8,128)S(1)}, f32[53,4,8,128]{3,2,1,0:T(8,128)}, u32[]{:S(2)}) %copy-start) | copy-done | bytes 868376
  1.2 0.0 copy-start.1
  1.2 0.2 shard_map.73
  1.3 2.1 %collective-permute-start.3 = (f32[424,128]{1,0:T(8,128)S(1)}, f32[424,128]{1,0:T(8,128)S(1)}, u32[]{:S(2)}, u32[]{:S(2)}) collective-permute-start(f32[424,128]{1,0:T(8,128)S(1)} %get-tuple-element.26), channel_id=1, source_target_pairs={{0,4},{4,0},{8,12},{12,8},{16,20},{20,16},{24,28},{28,24},{1,5},{5... | collective-permute-start | bytes 651272 | tf_op jit(solution)/shard_map/ppermute | solution.py:27
  3.4 1.0 %collective-permute-start = (f32[4,56,128]{2,1,0:T(8,128)S(1)}, f32[4,56,128]{2,1,0:T(8,128)S(1)}, u32[]{:S(2)}, u32[]{:S(2)}) collective-permute-start(f32[4,56,128]{2,1,0:T(8,128)S(1)} %get-tuple-element.21), channel_id=1, source_target_pairs={{0,1},{1,0},{2,3},{3,2},{4,5},{5,4},{6,7},{7,6},{8,9},{9,8},{10,11... | collective-permute-start | bytes 344072 | tf_op jit(solution)/shard_map/ppermute | solution.py:27
  4.4 0.0 copy-start.3
  4.4 0.0 copy-start.4
  4.4 3.2 %collective-permute-start.1 = (f32[4,56,128]{2,1,0:T(8,128)S(1)}, f32[4,56,128]{2,1,0:T(8,128)S(1)}, u32[]{:S(2)}, u32[]{:S(2)}) collective-permute-start(f32[4,56,128]{2,1,0:T(8,128)S(1)} %get-tuple-element.22), channel_id=1, source_target_pairs={{1,2},{2,1},{5,6},{6,5},{9,10},{10,9},{13,14},{14,13},{17,18},{18,... | collective-permute-start | bytes 344072 | tf_op jit(solution)/shard_map/ppermute | solution.py:27
  7.6 0.9 %copy.10.inverses = f32[4,53,53]{2,1,0:T(8,128)S(1)} copy(f32[4,53,53]{2,0,1:T(4,128)} %param.11) | data formatting | bytes 89888 | tf_op args[4]
  8.5 0.0 copy-start.2
  8.5 0.0 collective-permute-done.ya
  8.5 2.1 %collective-permute-done.1.yb = f32[4,56,128]{2,1,0:T(8,128)S(1)} collective-permute-done((f32[4,56,128]{2,1,0:T(8,128)S(1)}, f32[4,56,128]{2,1,0:T(8,128)S(1)}, u32[]{:S(2)}, u32[]{:S(2)}) %collective-permute-start.1) | collective-permute-done | bytes 114720 | tf_op jit(solution)/shard_map/ppermute | solution.py:27
  10.6 0.0 copy-done.1
  10.6 0.0 copy-done.3
  10.6 0.0 copy-done.4
  10.6 1.2 %shard_map.74 = (f32[4,8,56,128]{3,2,1,0:T(8,128)S(1)}, f32[56,128]{1,0:T(8,128)S(1)}, f32[856,128]{1,0:T(8,128)S(1)}) custom-call(f32[53]{0:T(128)S(1)} %copy-done.4, f32[1696,128]{1,0:T(8,128)S(1)} %bitcast.3, f32[4,56,128]{2,1,0:T(8,128)S(1)} %collective-permute-done.ya, f32[4,56,128]{2,1,0:T(8,128)S(1)} %collective-permute-done.1.yb, ...), custom_call_target="tpu_custom_call" | custom-call | flops 1000000000 | bytes 1 | tf_op jit(solution)/shard_map/pallas_call | solution.py:276
  11.9 0.7 %collective-permute-start.2 = (f32[856,128]{1,0:T(8,128)S(1)}, f32[856,128]{1,0:T(8,128)S(1)}, u32[]{:S(2)}, u32[]{:S(2)}) collective-permute-start(f32[856,128]{1,0:T(8,128)S(1)} %get-tuple-element.24), channel_id=1, source_target_pairs={{4,8},{8,4},{12,16},{16,12},{20,24},{24,20},{5,9},{9,5},{13,17},{1... | collective-permute-start | bytes 1314824 | tf_op jit(solution)/shard_map/ppermute | solution.py:27
  12.6 0.0 collective-permute-done.3.halo
  12.6 0.0 copy-start.5
  12.6 0.0 copy-start.6
  12.6 0.0 copy-done.2
  12.6 0.6 %copy-done.5 = f32[4]{0:T(128)S(1)} copy-done((f32[4]{0:T(128)S(1)}, f32[4]{0:T(128)}, u32[]{:S(2)}) %copy-start.5) | copy-done | bytes 40
  13.2 0.0 copy-done.6
  13.3 6.2 %shard_map.75 = (f32[4,8,56,128]{3,2,1,0:T(8,128)S(1)}, f32[4,8,56,128]{3,2,1,0:T(8,128)S(1)}, f32[424,128]{1,0:T(8,128)S(1)}, bf16[64,192]{1,0:T(8,128)(2,1)S(1)}, bf16[224,192]{1,0:T(8,128)(2,1)S(1)}) custom-call(f32[4]{0:T(128)S(1)} %copy-done.5, s32[4]{0:T(128)S(1)} %copy-done.6, f32[4,8,56,128]{3,2,1,0:T(8,128)S(1)} %get-tuple-element.23.s_ref, ...), custom_call_target="tpu_custom_call" | custom-call | flops 6000000000 | bytes 1 | tf_op jit(solution)/shard_map/pallas_call | solution.py:276
  19.4 3.8 %collective-permute-start.4 = (f32[424,128]{1,0:T(8,128)S(1)}, f32[424,128]{1,0:T(8,128)S(1)}, u32[]{:S(2)}, u32[]{:S(2)}) collective-permute-start(f32[424,128]{1,0:T(8,128)S(1)} %get-tuple-element.33), channel_id=1, source_target_pairs={{0,4},{4,0},{8,12},{12,8},{16,20},{20,16},{24,28},{28,24},{1,5},{5... | collective-permute-start | bytes 651272 | tf_op jit(solution)/shard_map/ppermute | solution.py:27
  23.2 0.0 collective-permute-done.2.message
  23.2 4.7 %shard_map.76 = (f32[4,8,56,128]{3,2,1,0:T(8,128)S(1)}, f32[4,8,56,128]{3,2,1,0:T(8,128)S(1)}, f32[8,56,128]{2,1,0:T(8,128)S(1)}, f32[4,56,128]{2,1,0:T(8,128)S(1)}, f32[4,56,128]{2,1,0:T(8,128)S(1)}) custom-call(f32[4]{0:T(128)S(1)} %copy-done.5, s32[4]{0:T(128)S(1)} %copy-done.6, ...), custom_call_target="tpu_custom_call", output_to_operand_aliasing={{0}: (10, {}), {1}: (11, {})} | custom-call | flops 4000000000 | bytes 1 | tf_op jit(solution)/shard_map/pallas_call | solution.py:276
  27.9 0.1 collective-permute-start.5
  28.0 3.6 %collective-permute-start.6 = (f32[4,56,128]{2,1,0:T(8,128)S(1)}, f32[4,56,128]{2,1,0:T(8,128)S(1)}, u32[]{:S(2)}, u32[]{:S(2)}) collective-permute-start(f32[4,56,128]{2,1,0:T(8,128)S(1)} %get-tuple-element.36), channel_id=1, source_target_pairs={{1,2},{2,1},{5,6},{6,5},{9,10},{10,9},{13,14},{14,13},{17,18},{18,... | collective-permute-start | bytes 344072 | tf_op jit(solution)/shard_map/ppermute | solution.py:27
  31.6 0.0 collective-permute-done.4.xa
  31.6 0.0 collective-permute-done.5.ya
  31.7 2.5 %collective-permute-done.6.yb = f32[4,56,128]{2,1,0:T(8,128)S(1)} collective-permute-done((f32[4,56,128]{2,1,0:T(8,128)S(1)}, f32[4,56,128]{2,1,0:T(8,128)S(1)}, u32[]{:S(2)}, u32[]{:S(2)}) %collective-permute-start.6) | collective-permute-done | bytes 114720 | tf_op jit(solution)/shard_map/ppermute | solution.py:27
  34.1 2.2 %shard_map.77 = f32[1696,128]{1,0:T(8,128)} custom-call(f32[4,8,56,128]{3,2,1,0:T(8,128)S(1)} %get-tuple-element.31.sec, f32[4,8,56,128]{3,2,1,0:T(8,128)S(1)} %get-tuple-element.32.f_ref, f32[424,128]{1,0:T(8,128)S(1)} %collective-permute-done.4.xa, f32[8,56,128]{2,1,0:T(8,128)S(1)} %get-tuple-element.34.beyond, ...), custom_call_target="tpu_custom_call" | custom-call | flops 2000000000 | bytes 1 | tf_op jit(solution)/shard_map/pallas_call | solution.py:276
Async XLA Ops:
  0.0 1.2 %copy-start = (f32[53,4,8,128]{3,2,1,0:T(8,128)S(1)}, f32[53,4,8,128]{3,2,1,0:T(8,128)}, u32[]{:S(2)}) copy-start(f32[53,4,8,128]{3,2,1,0:T(8,128)} %param.7) | copy-start | bytes 2605060
  1.2 9.5 %copy-start.1 = (f32[53,4,8,128]{3,2,1,0:T(8,128)S(1)}, f32[53,4,8,128]{3,2,1,0:T(8,128)}, u32[]{:S(2)}) copy-start(f32[53,4,8,128]{3,2,1,0:T(8,128)} %param.7) | copy-start | bytes 2605060
  1.3 11.2 %collective-permute-start.3 = (f32[424,128]{1,0:T(8,128)S(1)}, f32[424,128]{1,0:T(8,128)S(1)}, u32[]{:S(2)}, u32[]{:S(2)}) collective-permute-start(f32[424,128]{1,0:T(8,128)S(1)} %get-tuple-element.26), channel_id=1, source_target_pairs={{0,4},{4,0},{8,12},{12,8},{16,20},{20,16},{24,28},{28,24},{1,5},{5... | collective-permute-start | bytes 651272 | tf_op jit(solution)/shard_map/ppermute | solution.py:27
  3.4 5.0 %collective-permute-start = (f32[4,56,128]{2,1,0:T(8,128)S(1)}, f32[4,56,128]{2,1,0:T(8,128)S(1)}, u32[]{:S(2)}, u32[]{:S(2)}) collective-permute-start(f32[4,56,128]{2,1,0:T(8,128)S(1)} %get-tuple-element.21), channel_id=1, source_target_pairs={{0,1},{1,0},{2,3},{3,2},{4,5},{5,4},{6,7},{7,6},{8,9},{9,8},{10,11... | collective-permute-start | bytes 344072 | tf_op jit(solution)/shard_map/ppermute | solution.py:27
  4.4 6.2 %copy-start.3 = (s32[4,8,128]{2,1,0:T(8,128)S(1)}, s32[4,8,128]{2,1,0:T(8,128)}, u32[]{:S(2)}) copy-start(s32[4,8,128]{2,1,0:T(8,128)} %cls.5) | copy-start | bytes 49156
  4.4 6.2 %copy-start.4 = (f32[53]{0:T(128)S(1)}, f32[53]{0:T(128)}, u32[]{:S(2)}) copy-start(f32[53]{0:T(128)} %dif.1) | copy-start | bytes 640
  4.4 6.2 %collective-permute-start.1 = (f32[4,56,128]{2,1,0:T(8,128)S(1)}, f32[4,56,128]{2,1,0:T(8,128)S(1)}, u32[]{:S(2)}, u32[]{:S(2)}) collective-permute-start(f32[4,56,128]{2,1,0:T(8,128)S(1)} %get-tuple-element.22), channel_id=1, source_target_pairs={{1,2},{2,1},{5,6},{6,5},{9,10},{10,9},{13,14},{14,13},{17,18},{18,... | collective-permute-start | bytes 344072 | tf_op jit(solution)/shard_map/ppermute | solution.py:27
  8.5 4.1 %copy-start.2 = (f32[53,53]{1,0:T(8,128)S(1)}, f32[53,53]{1,0:T(8,128)}, u32[]{:S(2)}) copy-start(f32[53,53]{1,0:T(8,128)} %mixing.1) | copy-start | bytes 33712
  11.9 11.3 %collective-permute-start.2 = (f32[856,128]{1,0:T(8,128)S(1)}, f32[856,128]{1,0:T(8,128)S(1)}, u32[]{:S(2)}, u32[]{:S(2)}) collective-permute-start(f32[856,128]{1,0:T(8,128)S(1)} %get-tuple-element.24), channel_id=1, source_target_pairs={{4,8},{8,4},{12,16},{16,12},{20,24},{24,20},{5,9},{9,5},{13,17},{1... | collective-permute-start | bytes 1314824 | tf_op jit(solution)/shard_map/ppermute | solution.py:27
  12.6 0.7 %copy-start.5 = (f32[4]{0:T(128)S(1)}, f32[4]{0:T(128)}, u32[]{:S(2)}) copy-start(f32[4]{0:T(128)} %rate.3) | copy-start | bytes 52
  12.6 0.7 %copy-start.6 = (s32[4]{0:T(128)S(1)}, s32[4]{0:T(128)}, u32[]{:S(2)}) copy-start(s32[4]{0:T(128)} %count.3) | copy-start | bytes 52
  19.4 12.2 %collective-permute-start.4 = (f32[424,128]{1,0:T(8,128)S(1)}, f32[424,128]{1,0:T(8,128)S(1)}, u32[]{:S(2)}, u32[]{:S(2)}) collective-permute-start(f32[424,128]{1,0:T(8,128)S(1)} %get-tuple-element.33), channel_id=1, source_target_pairs={{0,4},{4,0},{8,12},{12,8},{16,20},{20,16},{24,28},{28,24},{1,5},{5... | collective-permute-start | bytes 651272 | tf_op jit(solution)/shard_map/ppermute | solution.py:27
  27.9 3.7 %collective-permute-start.5 = (f32[4,56,128]{2,1,0:T(8,128)S(1)}, f32[4,56,128]{2,1,0:T(8,128)S(1)}, u32[]{:S(2)}, u32[]{:S(2)}) collective-permute-start(f32[4,56,128]{2,1,0:T(8,128)S(1)} %get-tuple-element.35), channel_id=1, source_target_pairs={{0,1},{1,0},{2,3},{3,2},{4,5},{5,4},{6,7},{7,6},{8,9},{9,8},{10,11... | collective-permute-start | bytes 344072 | tf_op jit(solution)/shard_map/ppermute | solution.py:27
  28.0 6.1 %collective-permute-start.6 = (f32[4,56,128]{2,1,0:T(8,128)S(1)}, f32[4,56,128]{2,1,0:T(8,128)S(1)}, u32[]{:S(2)}, u32[]{:S(2)}) collective-permute-start(f32[4,56,128]{2,1,0:T(8,128)S(1)} %get-tuple-element.36), channel_id=1, source_target_pairs={{1,2},{2,1},{5,6},{6,5},{9,10},{10,9},{13,14},{14,13},{17,18},{18,... | collective-permute-start | bytes 344072 | tf_op jit(solution)/shard_map/ppermute | solution.py:27

commit v2 on v1

--- a/solution.py
+++ b/solution.py
@@ -24,6 +24,12 @@
     pairs = []
     for i in range(first, count - 1, 2):
         pairs += [(i, i + 1), (i + 1, i)]
+    return lax.ppermute(block, axis, pairs)
+
+
+def hand_on(block, axis):
+    count = lax.axis_size(axis)
+    pairs = [(i, i + 2) for i in range(0, count - 2, 2)] + [(i, i - 2) for i in range(3, count, 2)]
     return lax.ppermute(block, axis, pairs)
 
 
@@ -120,13 +126,22 @@
     kind_ref[i] = kind
 
 
-def faces_kernel(nx, ny, ns, block, fa, fya, fyb):
-    xa = near_index("gx", nx)
+def exists(axis):
+    me, last = lax.axis_index(axis), lax.axis_size(axis) - 1
+    return jnp.where(me % 2 == 0, me > 0, me < last)
+
+
+def faces_kernel(nx, ny, ns, rate, count, dif, block, cls, mixing, fa, fy):
+    xa, far = near_index("gx", nx), far_index("gx", nx)
     for s in range(ns):
         fa[pl.ds(s * ny, ny), :] = block[pl.ds(s * nx * ny + xa * ny, ny), :]
-    for face, y in ((fya, near_index("gy", ny)), (fyb, far_index("gy", ny))):
+    for k, index in enumerate((near_index, far_index)):
+        y, inner = index("gy", ny), index("gy", ny, 1)
+        first = k * (nx + 1)
         for x in range(nx):
-            put(face, (x,), block[pl.ds(x * ny + y, ns, stride=nx * ny), :], ns)
+            put(fy, (first + x,), block[pl.ds(x * ny + y, ns, stride=nx * ny), :], ns)
+        put(fy, (first + nx,), block[pl.ds(far * ny + inner, ns, stride=nx * ny), :], ns)
+        fy[first + nx, ns : ns + 1, :] = cls[far, pl.ds(y, 1), :].astype(F32)
 
 
 def make_scale(scale, dif, ns):
@@ -159,18 +174,22 @@
     w2[:, 2 * deep :] = widen(jnp.concatenate(lows, axis=0), whole).astype(BF16)[:, :deep]
 
 
+def prep_kernel(nx, ny, ns, nclass, rate, dif, block, mixing, inverses, s_ref, scale, w1, w2, square):
+    make_scale(scale, dif, ns)
+    make_weights(w1, w2, square, mixing, inverses, rate, ns, s_ref.shape[2], nclass)
+    for x in range(nx):
+        for y in range(ny):
+            put(s_ref, (x, y), block[pl.ds(x * ny + y, ns, stride=nx * ny), :], ns)
+
+
 def edge_rows(ya, yb):
     even_y = lax.axis_index("gy") % 2 == 0
     return lambda x, high: jnp.where(even_y == high, ya[x], yb[x])
 
 
-def send_kernel(nx, ny, ns, dif, block, ya, yb, cls, s_ref, scale, message):
-    make_scale(scale, dif, ns)
+def send_kernel(nx, ny, ns, block, s_ref, ya, yb, cls, scale, message):
     far, inner = far_index("gx", nx), far_index("gx", nx, 1)
     edge = edge_rows(ya, yb)
-    for x in range(nx):
-        for y in range(ny):
-            put(s_ref, (x, y), block[pl.ds(x * ny + y, ns, stride=nx * ny), :], ns)
     for s in range(ns):
         message[pl.ds(s * ny, ny), :] = block[pl.ds(s * nx * ny + far * ny, ny), :]
     for y in range(ny):
@@ -179,15 +198,17 @@
         high = s_ref[far, y + 1] if y < ny - 1 else edge(far, True)
         part = v + scale[...] * lap(v, [s_ref[inner, y], low, high])
         message[pl.ds(ns * ny + y, ns, stride=ny), :] = part[:ns]
-    message[pl.ds(2 * ns * ny, ny), :] = cls[far].astype(F32)
-
-
-def near_kernel(nx, ny, ns, nclass, rate, count, s_ref, halo, ya, yb, mixing, inverses, cls, scale,
-                f_ref, sec, face, w1, w2, y_ref, st_ref, r1_ref, kind_ref, square):
-    sp = s_ref.shape[2]
-    make_weights(w1, w2, square, mixing, inverses, rate, ns, sp, nclass)
+    base = 2 * ns * ny
+    message[pl.ds(base, ny), :] = cls[far].astype(F32)
+    message[pl.ds(base + ny, ns, stride=2), :] = ya[far][:ns]
+    message[pl.ds(base + ny + 1, ns, stride=2), :] = yb[far][:ns]
+
+
+def near_kernel(nx, ny, ns, nclass, rate, count, s_ref, halo, ya, yb, cls, scale, w1, w2,
+                f_ref, sec, face, fy, y_ref, st_ref, r1_ref, kind_ref):
+    sp, nz = s_ref.shape[2:]
     edge = edge_rows(ya, yb)
-    near, inner = near_index("gx", nx), near_index("gx", nx, 1)
+    near, inner, far = near_index("gx", nx), near_index("gx", nx, 1), far_index("gx", nx)
     places = [(near, y) for y in range(ny)] + [(x, y) for x in range(1, nx - 1) for y in range(ny)]
     for i, (x, y) in enumerate(places):
         if i < ny:
@@ -205,15 +226,23 @@
         sec[x, y] = y_ref[i]
         if i < ny:
             face[pl.ds(y, ns, stride=ny), :] = y_ref[i][:ns]
+    for k, y in enumerate((near_index("gy", ny), far_index("gy", ny))):
+        fy[k * nx + far] = jnp.zeros((sp, nz), F32)
+        fy[k * nx + near] = sec[near, y]
+        for x in range(1, nx - 1):
+            fy[k * nx + x] = sec[x, y]
 
 
 def far_kernel(nx, ny, ns, nclass, rate, count, s_ref, message, ya, yb, cls, scale, w1, w2, f_in, sec_in,
-               f_ref, sec, beyond, fya, fyb, y_ref, st_ref, r1_ref, kind_ref):
+               f_ref, sec, beyond, beside, y_ref, st_ref, r1_ref, kind_ref):
     sp = s_ref.shape[2]
     edge = edge_rows(ya, yb)
     far, inner = far_index("gx", nx), far_index("gx", nx, 1)
-    me, last = lax.axis_index("gx"), lax.axis_size("gx") - 1
-    has = jnp.where(me % 2 == 0, me > 0, me < last)
+    base = 2 * ns * ny
+
+    def begin(i, target, kind):
+        start_row(i, target, kind, rate, y_ref, st_ref, r1_ref, kind_ref, nclass)
+
     for y in range(ny):
         v = s_ref[far, y]
         nbrs = [
@@ -224,27 +253,38 @@
         ]
         force = scale[...] * lap(v, nbrs)
         f_ref[far, y] = force
-        start_row(y, v + force, cls[far, y : y + 1, :], rate, y_ref, st_ref, r1_ref, kind_ref, nclass)
+        begin(y, v + force, cls[far, y : y + 1, :])
         target = widen(message[pl.ds(ns * ny + y, ns, stride=ny), :], sp) + scale[...] * v
-        kind = message[pl.ds(2 * ns * ny + y, 1), :].astype(jnp.int32)
-        start_row(ny + y, target, kind, rate, y_ref, st_ref, r1_ref, kind_ref, nclass)
-    newton(2 * ny, y_ref, st_ref, r1_ref, kind_ref, count, w1, w2, nclass)
+        begin(ny + y, target, message[pl.ds(base + y, 1), :].astype(jnp.int32))
+    for k, (halo, y) in enumerate(((ya, near_index("gy", ny)), (yb, far_index("gy", ny)))):
+        v = halo[far]
+        corner = widen(message[pl.ds(base + ny + k, ns, stride=2), :], sp)
+        target = v + scale[...] * lap(v, [halo[inner], corner, halo[nx], s_ref[far, y]])
+        begin(2 * ny + k, target, halo[nx, ns : ns + 1, :].astype(jnp.int32))
+    newton(2 * ny + 2, y_ref, st_ref, r1_ref, kind_ref, count, w1, w2, nclass)
+    there = exists("gx")
     for y in range(ny):
         sec[far, y] = y_ref[y]
-        beyond[y] = jnp.where(has, y_ref[ny + y], 0.0)
-    for out, y in ((fya, near_index("gy", ny)), (fyb, far_index("gy", ny))):
-        for x in range(nx):
-            out[x] = sec[x, y]
-
-
-def last_kernel(nx, ny, ns, sec, f_ref, xa, beyond, ya, yb, scale, out):
+        beyond[y] = jnp.where(there, y_ref[ny + y], 0.0)
+    beside[0] = y_ref[2 * ny]
+    beside[1] = jnp.where(exists("gy"), y_ref[2 * ny + 1], 0.0)
+
+
+def last_kernel(nx, ny, ns, sec, f_ref, xa, beyond, ya, yb, beside, scale, out):
     sp = sec.shape[2]
     even_x = lax.axis_index("gx") % 2 == 0
-    edge = edge_rows(ya, yb)
+    even_y = lax.axis_index("gy") % 2 == 0
 
     def outer(y, high):
         near = widen(xa[pl.ds(y, ns, stride=ny), :], sp)
         return jnp.where(even_x == high, near, beyond[y])
+
+    def edge(x, high):
+        value = jnp.where(even_y == high, ya[x], yb[x])
+        if 0 < x < nx - 1:
+            return value
+        side = jnp.where(even_y == high, beside[0], beside[1])
+        return jnp.where(even_x == (x == 0), side, value)
 
     for x in range(nx):
         for y in range(ny):
@@ -262,7 +302,8 @@
 def local(species, diffusion, class_rate, mixing, inverses, newton_counts, cell_class):
     ns, nx, ny, nz = species.shape
     nclass = class_rate.shape[0]
-    sp, deep = up(ns, SUB), up(ns, 16)
+    sp = up(ns + 1, SUB)
+    deep = up(sp, 16)
     block = species.reshape(ns * nx * ny, nz)
 
     def shape(*dims, dtype=F32):
@@ -270,7 +311,6 @@
 
     field = shape(nx, ny, sp, nz)
     xface = shape(ns * ny, nz)
-    yface = shape(nx, sp, nz)
 
     def call(kernel, small, big, outs, scratch=(), mib=6, work=1, alias=()):
         return pl.pallas_call(
@@ -293,44 +333,59 @@
         ]
 
     us = 10**9
-    fa, fya, fyb = call(functools.partial(faces_kernel, nx, ny, ns), [], [block], [xface, yface, yface])
+    part = functools.partial
+    rate, count = class_rate, newton_counts
+    fa, fy = call(
+        part(faces_kernel, nx, ny, ns),
+        [rate, count, diffusion],
+        [block, cell_class, mixing],
+        [xface, shape(2 * (nx + 1), sp, nz)],
+    )
+    hya = swap(fy, "gy", 0)
     ha = swap(fa, "gx", 0)
-    hya = swap(fya, "gy", 0)
-    hyb = swap(fyb, "gy", 1)
-    s_ref, scale, message = call(
-        functools.partial(send_kernel, nx, ny, ns),
-        [diffusion],
-        [block, hya, hyb, cell_class],
-        [field, shape(sp, nz), shape(2 * ns * ny + ny, nz)],
+    hyb = hand_on(hya[nx + 1 :], "gy")
+    s_ref, scale, w1, w2 = call(
+        part(prep_kernel, nx, ny, ns, nclass),
+        [rate, diffusion],
+        [block, mixing, inverses],
+        [field, shape(sp, nz), shape(deep, 3 * deep, dtype=BF16), shape(up(nclass * sp, 16), 3 * deep, dtype=BF16)],
+        [pltpu.VMEM((deep, 2 * deep), F32)],
         work=us,
     )
+    (message,) = call(
+        part(send_kernel, nx, ny, ns),
+        [],
+        [block, s_ref, hya, hyb, cell_class, scale],
+        [shape(2 * ns * ny + ny + 2 * ns, nz)],
+        work=us // 2,
+    )
     message = swap(message, "gx", 1)
-    force, sec, fa, w1, w2 = call(
-        functools.partial(near_kernel, nx, ny, ns, nclass),
-        [class_rate, newton_counts],
-        [s_ref, ha, hya, hyb, mixing, inverses, cell_class, scale],
-        [field, field, xface, shape(deep, 3 * deep, dtype=BF16), shape(up(nclass * sp, 16), 3 * deep, dtype=BF16)],
-        scratch((nx - 1) * ny) + [pltpu.VMEM((deep, 2 * deep), F32)],
+    force, sec, fa, fy = call(
+        part(near_kernel, nx, ny, ns, nclass),
+        [rate, count],
+        [s_ref, ha, hya, hyb, cell_class, scale, w1, w2],
+        [field, field, xface, shape(2 * nx, sp, nz)],
+        scratch((nx - 1) * ny),
         mib=14,
         work=6 * us,
     )
+    back_ya = swap(fy, "gy", 0)
     ha = swap(fa, "gx", 0)
-    force, sec, beyond, fya, fyb = call(
-        functools.partial(far_kernel, nx, ny, ns, nclass),
-        [class_rate, newton_counts],
+    back_yb = hand_on(back_ya[nx:], "gy")
+    force, sec, beyond, beside = call(
+        part(far_kernel, nx, ny, ns, nclass),
+        [rate, count],
         [s_ref, message, hya, hyb, cell_class, scale, w1, w2, force, sec],
-        [field, field, shape(ny, sp, nz), yface, yface],
-        scratch(2 * ny),
+        [field, field, shape(ny, sp, nz), shape(2, sp, nz)],
+        scratch(2 * ny + 2),
         mib=12,
-        work=4 * us,
+        work=5 * us,
         alias=((10, 0), (11, 1)),
     )
-    hya = swap(fya, "gy", 0)
-    hyb = swap(fyb, "gy", 1)
     (out,) = call(
-        functools.partial(last_kernel, nx, ny, ns),
+        part(last_kernel, nx, ny, ns),
         [],
-        [sec, force, ha, beyond, hya, hyb, scale],
+        [sec, force, ha, beyond, back_ya, back_yb, beside, scale],
         [shape(*block.shape)],
         work=2 * us,
     )

time: 36.6 us -> 37 us (1.011)
  the two profiles are of different devices: /device:TPU:1 before, /device:TPU:0 now
where the time goes in v2:
time: 37 us; the launch traced here: 36.6 us
  starting transfers between devices  16 us (43%)
  Pallas kernels  15.8 us (43%)
  local copies, waits for them, and re-layouts  3.36 us (9%)
  waiting for transfers between devices  1.33 us (4%)
    pallas_call x6, Pallas kernels, call(): pl.pallas_call(kernel, out_shape=tuple(outs), in_specs=[SMEM] * len(small...  15.8 us
    ppermute x5, starting transfers between devices, swap(): return lax.ppermute(block, axis, pairs)  8.2 us
    ppermute x2, starting transfers between devices, hand_on(): return lax.ppermute(block, axis, pairs)  7.8 us
    unnamed x21, local copies, waits for them, and re-layouts  3.34 us
    ppermute x2, waiting for transfers between devices, hand_on(): return lax.ppermute(block, axis, pairs)  1.32 us
  transfers between devices with their start and end apart: 7, of which 1 were waited for; matrix products, arithmetic and copies ran while one was open for 0% of the time, Pallas kernels for 35%

profile of v2, /device:TPU:0, one launch (start us, length us, event | category | flops | bytes accessed | tf_op | source)
XLA Modules:
  0.0 36.6 jit_solution(17952350698385272809)
XLA Ops:
  0.0 0.0 copy-start.7
  0.0 0.0 copy-start.8
  0.0 0.0 copy-start.6
  0.0 0.6 %copy-done.7 = f32[4]{0:T(128)S(1)} copy-done((f32[4]{0:T(128)S(1)}, f32[4]{0:T(128)}, u32[]{:S(2)}) %copy-start.7) | copy-done | bytes 40
  0.7 0.0 copy-done.8
  0.7 0.0 copy-done.6
  0.7 0.0 copy-start
  0.7 1.2 %copy-done = f32[53,4,8,128]{3,2,1,0:T(8,128)S(1)} copy-done((f32[53,4,8,128]{3,2,1,0:T(8,128)S(1)}, f32[53,4,8,128]{3,2,1,0:T(8,128)}, u32[]{:S(2)}) %copy-start) | copy-done | bytes 868376
  1.9 0.0 copy-start.2
  1.9 0.7 %copy-done.2 = s32[4,8,128]{2,1,0:T(8,128)S(1)} copy-done((s32[4,8,128]{2,1,0:T(8,128)S(1)}, s32[4,8,128]{2,1,0:T(8,128)}, u32[]{:S(2)}) %copy-start.2) | copy-done | bytes 16408
  2.6 0.0 copy-start.4
  2.6 0.7 %copy-done.4 = f32[53,53]{1,0:T(8,128)S(1)} copy-done((f32[53,53]{1,0:T(8,128)S(1)}, f32[53,53]{1,0:T(8,128)}, u32[]{:S(2)}) %copy-start.4) | copy-done | bytes 11260
  3.3 0.0 copy-start.1
  3.3 0.8 %shard_map.74 = (f32[424,128]{1,0:T(8,128)S(1)}, f32[10,56,128]{2,1,0:T(8,128)S(1)}) custom-call(f32[4]{0:T(128)S(1)} %copy-done.7, s32[4]{0:T(128)S(1)} %copy-done.8, f32[53]{0:T(128)S(1)} %copy-done.6, f32[1696,128]{1,0:T(8,128)S(1)} %bitcast.2, s32[4,8,128]{2,1,0:T(8,128)S(1)} %copy-done.2, f32[53,53]{1,0:T(8,128)S(1)} %copy-done.4), custom_call_target="tpu_custom_call" | custom-call | flops 1 | bytes 1 | tf_op jit(solution)/shard_map/pallas_call | solution.py:316
  4.1 0.6 %collective-permute-start = (f32[10,56,128]{2,1,0:T(8,128)S(1)}, f32[10,56,128]{2,1,0:T(8,128)S(1)}, u32[]{:S(2)}, u32[]{:S(2)}) collective-permute-start(f32[10,56,128]{2,1,0:T(8,128)S(1)} %get-tuple-element.20), channel_id=1, source_target_pairs={{0,1},{1,0},{2,3},{3,2},{4,5},{5,4},{6,7},{7,6},{8,9},{9,8},{10,11... | collective-permute-start | bytes 860168 | tf_op jit(solution)/shard_map/ppermute | solution.py:27
  4.7 0.0 copy-start.9
  4.7 2.6 %collective-permute-start.3 = (f32[424,128]{1,0:T(8,128)S(1)}, f32[424,128]{1,0:T(8,128)S(1)}, u32[]{:S(2)}, u32[]{:S(2)}) collective-permute-start(f32[424,128]{1,0:T(8,128)S(1)} %get-tuple-element.24), channel_id=1, source_target_pairs={{0,4},{4,0},{8,12},{12,8},{16,20},{20,16},{24,28},{28,24},{1,5},{5... | collective-permute-start | bytes 651272 | tf_op jit(solution)/shard_map/ppermute | solution.py:27
  7.2 0.0 collective-permute-done.ya
  7.2 0.0 copy-start.5
  7.3 3.4 %collective-permute-start.1 = (f32[5,56,128]{2,1,0:T(8,128)S(1)}, f32[5,56,128]{2,1,0:T(8,128)S(1)}, u32[]{:S(2)}, u32[]{:S(2)}) collective-permute-start(f32[5,56,128]{2,1,0:T(8,128)S(1)} %slice.8), channel_id=1, source_target_pairs={{0,2},{3,1},{4,6},{7,5},{8,10},{11,9},{12,14},{15,13},{16,18},{19,... | collective-permute-start | bytes 430088 | tf_op jit(solution)/shard_map/ppermute | solution.py:33
  10.7 0.0 copy-done.9
  10.7 0.0 copy-done.1
  10.7 0.0 copy-done.5
  10.7 0.0 copy-start.3
  10.8 1.2 %shard_map.73 = (f32[4,8,56,128]{3,2,1,0:T(8,128)S(1)}, f32[56,128]{1,0:T(8,128)S(1)}, bf16[64,192]{1,0:T(8,128)(2,1)S(1)}, bf16[224,192]{1,0:T(8,128)(2,1)S(1)}) custom-call(f32[4]{0:T(128)S(1)} %copy-done.7, f32[53]{0:T(128)S(1)} %copy-done.6, f32[1696,128]{1,0:T(8,128)S(1)} %bitcast.3, f32[53,53]{1,0:T(8,128)S(1)} %copy-done.5, ...), custom_call_target="tpu_custom_call" | custom-call | flops 1000000000 | bytes 1 | tf_op jit(solution)/shard_map/pallas_call | solution.py:316
  12.0 1.3 %collective-permute-done.1.yb = f32[5,56,128]{2,1,0:T(8,128)S(1)} collective-permute-done((f32[5,56,128]{2,1,0:T(8,128)S(1)}, f32[5,56,128]{2,1,0:T(8,128)S(1)}, u32[]{:S(2)}, u32[]{:S(2)}) %collective-permute-start.1) | collective-permute-done | bytes 143392 | tf_op jit(solution)/shard_map/ppermute | solution.py:33
  13.3 0.0 copy-done.3
  13.3 0.2 shard_map.75
  13.5 0.7 %collective-permute-start.2 = (f32[962,128]{1,0:T(8,128)S(1)}, f32[962,128]{1,0:T(8,128)S(1)}, u32[]{:S(2)}, u32[]{:S(2)}) collective-permute-start(f32[962,128]{1,0:T(8,128)S(1)} %shard_map.75), channel_id=1, source_target_pairs={{4,8},{8,4},{12,16},{16,12},{20,24},{24,20},{5,9},{9,5},{13,17},{1... | collective-permute-start | bytes 1477640 | tf_op jit(solution)/shard_map/ppermute | solution.py:27
  14.2 0.0 collective-permute-done.3.halo
  14.3 6.1 %shard_map.76 = (f32[4,8,56,128]{3,2,1,0:T(8,128)S(1)}, f32[4,8,56,128]{3,2,1,0:T(8,128)S(1)}, f32[424,128]{1,0:T(8,128)S(1)}, f32[8,56,128]{2,1,0:T(8,128)S(1)}) custom-call(f32[4]{0:T(128)S(1)} %copy-done.7, s32[4]{0:T(128)S(1)} %copy-done.8, f32[4,8,56,128]{3,2,1,0:T(8,128)S(1)} %get-tuple-element.19.s_ref, f32[424,128]{1,0:T(8,128)S(1)} %collective-permute-done.3.halo, ...), custom_call_target="tpu_custom_call" | custom-call | flops 6000000000 | bytes 1 | tf_op jit(solution)/shard_map/pallas_call | solution.py:316
  20.4 0.1 collective-permute-start.5
  20.5 4.3 %collective-permute-start.4 = (f32[424,128]{1,0:T(8,128)S(1)}, f32[424,128]{1,0:T(8,128)S(1)}, u32[]{:S(2)}, u32[]{:S(2)}) collective-permute-start(f32[424,128]{1,0:T(8,128)S(1)} %get-tuple-element.29), channel_id=1, source_target_pairs={{0,4},{4,0},{8,12},{12,8},{16,20},{20,16},{24,28},{28,24},{1,5},{5... | collective-permute-start | bytes 651272 | tf_op jit(solution)/shard_map/ppermute | solution.py:27
  24.8 0.0 collective-permute-done.5.ya
  24.8 4.4 %collective-permute-start.6 = (f32[4,56,128]{2,1,0:T(8,128)S(1)}, f32[4,56,128]{2,1,0:T(8,128)S(1)}, u32[]{:S(2)}, u32[]{:S(2)}) collective-permute-start(f32[4,56,128]{2,1,0:T(8,128)S(1)} %slice.9), channel_id=1, source_target_pairs={{0,2},{3,1},{4,6},{7,5},{8,10},{11,9},{12,14},{15,13},{16,18},{19,... | collective-permute-start | bytes 344072 | tf_op jit(solution)/shard_map/ppermute | solution.py:33
  29.2 0.0 collective-permute-done.2.message
  29.2 5.2 %shard_map.77 = (f32[4,8,56,128]{3,2,1,0:T(8,128)S(1)}, f32[4,8,56,128]{3,2,1,0:T(8,128)S(1)}, f32[8,56,128]{2,1,0:T(8,128)S(1)}, f32[2,56,128]{2,1,0:T(8,128)S(1)}) custom-call(f32[4]{0:T(128)S(1)} %copy-done.7, s32[4]{0:T(128)S(1)} %copy-done.8, f32[4,8,56,128]{3,2,1,0:T(8,128)S(1)} %get-tuple-element.19.s_ref, ...), custom_call_target="tpu_custom_call", output_to_operand_aliasing={{0}: (10, {}), {1}: (11, {})} | custom-call | flops 5000000000 | bytes 1 | tf_op jit(solution)/shard_map/pallas_call | solution.py:316
  34.4 0.0 collective-permute-done.4.xa
  34.4 0.0 collective-permute-done.6.yb
  34.4 2.2 %shard_map.78 = f32[1696,128]{1,0:T(8,128)} custom-call(f32[4,8,56,128]{3,2,1,0:T(8,128)S(1)} %get-tuple-element.27.sec, f32[4,8,56,128]{3,2,1,0:T(8,128)S(1)} %get-tuple-element.28.f_ref, f32[424,128]{1,0:T(8,128)S(1)} %collective-permute-done.4.xa, f32[8,56,128]{2,1,0:T(8,128)S(1)} %get-tuple-element.30.beyond, ...), custom_call_target="tpu_custom_call" | custom-call | flops 2000000000 | bytes 1 | tf_op jit(solution)/shard_map/pallas_call | solution.py:316
  (3 shorter events, 0.0 us)
Async XLA Ops:
  0.0 0.7 %copy-start.7 = (f32[4]{0:T(128)S(1)}, f32[4]{0:T(128)}, u32[]{:S(2)}) copy-start(f32[4]{0:T(128)} %rate.7) | copy-start | bytes 52
  0.0 0.7 %copy-start.8 = (s32[4]{0:T(128)S(1)}, s32[4]{0:T(128)}, u32[]{:S(2)}) copy-start(s32[4]{0:T(128)} %count.5) | copy-start | bytes 52
  0.0 0.7 %copy-start.6 = (f32[53]{0:T(128)S(1)}, f32[53]{0:T(128)}, u32[]{:S(2)}) copy-start(f32[53]{0:T(128)} %dif.3) | copy-start | bytes 640
  0.7 1.2 %copy-start = (f32[53,4,8,128]{3,2,1,0:T(8,128)S(1)}, f32[53,4,8,128]{3,2,1,0:T(8,128)}, u32[]{:S(2)}) copy-start(f32[53,4,8,128]{3,2,1,0:T(8,128)} %param.7) | copy-start | bytes 2605060
  1.9 0.7 %copy-start.2 = (s32[4,8,128]{2,1,0:T(8,128)S(1)}, s32[4,8,128]{2,1,0:T(8,128)}, u32[]{:S(2)}) copy-start(s32[4,8,128]{2,1,0:T(8,128)} %cls.7) | copy-start | bytes 49156
  2.6 0.7 %copy-start.4 = (f32[53,53]{1,0:T(8,128)S(1)}, f32[53,53]{1,0:T(8,128)}, u32[]{:S(2)}) copy-start(f32[53,53]{1,0:T(8,128)} %mixing.3) | copy-start | bytes 33712
  3.3 7.4 %copy-start.1 = (f32[53,4,8,128]{3,2,1,0:T(8,128)S(1)}, f32[53,4,8,128]{3,2,1,0:T(8,128)}, u32[]{:S(2)}) copy-start(f32[53,4,8,128]{3,2,1,0:T(8,128)} %param.7) | copy-start | bytes 2605060
  4.1 3.1 %collective-permute-start = (f32[10,56,128]{2,1,0:T(8,128)S(1)}, f32[10,56,128]{2,1,0:T(8,128)S(1)}, u32[]{:S(2)}, u32[]{:S(2)}) collective-permute-start(f32[10,56,128]{2,1,0:T(8,128)S(1)} %get-tuple-element.20), channel_id=1, source_target_pairs={{0,1},{1,0},{2,3},{3,2},{4,5},{5,4},{6,7},{7,6},{8,9},{9,8},{10,11... | collective-permute-start | bytes 860168 | tf_op jit(solution)/shard_map/ppermute | solution.py:27
  4.7 6.0 %copy-start.9 = (f32[4,53,53]{2,0,1:T(4,128)S(1)}, f32[4,53,53]{2,0,1:T(4,128)}, u32[]{:S(2)}) copy-start(f32[4,53,53]{2,0,1:T(4,128)} %param.11) | copy-start | bytes 134836
  4.7 9.6 %collective-permute-start.3 = (f32[424,128]{1,0:T(8,128)S(1)}, f32[424,128]{1,0:T(8,128)S(1)}, u32[]{:S(2)}, u32[]{:S(2)}) collective-permute-start(f32[424,128]{1,0:T(8,128)S(1)} %get-tuple-element.24), channel_id=1, source_target_pairs={{0,4},{4,0},{8,12},{12,8},{16,20},{20,16},{24,28},{28,24},{1,5},{5... | collective-permute-start | bytes 651272 | tf_op jit(solution)/shard_map/ppermute | solution.py:27
  7.2 3.5 %copy-start.5 = (f32[53,53]{1,0:T(8,128)S(1)}, f32[53,53]{1,0:T(8,128)}, u32[]{:S(2)}) copy-start(f32[53,53]{1,0:T(8,128)} %mixing.3) | copy-start | bytes 33712
  7.3 6.1 %collective-permute-start.1 = (f32[5,56,128]{2,1,0:T(8,128)S(1)}, f32[5,56,128]{2,1,0:T(8,128)S(1)}, u32[]{:S(2)}, u32[]{:S(2)}) collective-permute-start(f32[5,56,128]{2,1,0:T(8,128)S(1)} %slice.8), channel_id=1, source_target_pairs={{0,2},{3,1},{4,6},{7,5},{8,10},{11,9},{12,14},{15,13},{16,18},{19,... | collective-permute-start | bytes 430088 | tf_op jit(solution)/shard_map/ppermute | solution.py:33
  10.7 2.6 %copy-start.3 = (s32[4,8,128]{2,1,0:T(8,128)S(1)}, s32[4,8,128]{2,1,0:T(8,128)}, u32[]{:S(2)}) copy-start(s32[4,8,128]{2,1,0:T(8,128)} %cls.7) | copy-start | bytes 49156
  13.5 15.6 %collective-permute-start.2 = (f32[962,128]{1,0:T(8,128)S(1)}, f32[962,128]{1,0:T(8,128)S(1)}, u32[]{:S(2)}, u32[]{:S(2)}) collective-permute-start(f32[962,128]{1,0:T(8,128)S(1)} %shard_map.75), channel_id=1, source_target_pairs={{4,8},{8,4},{12,16},{16,12},{20,24},{24,20},{5,9},{9,5},{13,17},{1... | collective-permute-start | bytes 1477640 | tf_op jit(solution)/shard_map/ppermute | solution.py:27
  20.4 4.4 %collective-permute-start.5 = (f32[8,56,128]{2,1,0:T(8,128)S(1)}, f32[8,56,128]{2,1,0:T(8,128)S(1)}, u32[]{:S(2)}, u32[]{:S(2)}) collective-permute-start(f32[8,56,128]{2,1,0:T(8,128)S(1)} %get-tuple-element.31), channel_id=1, source_target_pairs={{0,1},{1,0},{2,3},{3,2},{4,5},{5,4},{6,7},{7,6},{8,9},{9,8},{10,11... | collective-permute-start | bytes 688136 | tf_op jit(solution)/shard_map/ppermute | solution.py:27
  20.5 14.0 %collective-permute-start.4 = (f32[424,128]{1,0:T(8,128)S(1)}, f32[424,128]{1,0:T(8,128)S(1)}, u32[]{:S(2)}, u32[]{:S(2)}) collective-permute-start(f32[424,128]{1,0:T(8,128)S(1)} %get-tuple-element.29), channel_id=1, source_target_pairs={{0,4},{4,0},{8,12},{12,8},{16,20},{20,16},{24,28},{28,24},{1,5},{5... | collective-permute-start | bytes 651272 | tf_op jit(solution)/shard_map/ppermute | solution.py:27
  24.8 9.6 %collective-permute-start.6 = (f32[4,56,128]{2,1,0:T(8,128)S(1)}, f32[4,56,128]{2,1,0:T(8,128)S(1)}, u32[]{:S(2)}, u32[]{:S(2)}) collective-permute-start(f32[4,56,128]{2,1,0:T(8,128)S(1)} %slice.9), channel_id=1, source_target_pairs={{0,2},{3,1},{4,6},{7,5},{8,10},{11,9},{12,14},{15,13},{16,18},{19,... | collective-permute-start | bytes 344072 | tf_op jit(solution)/shard_map/ppermute | solution.py:33

commit v3 on v2

--- a/solution.py
+++ b/solution.py
@@ -27,12 +27,6 @@
     return lax.ppermute(block, axis, pairs)
 
 
-def hand_on(block, axis):
-    count = lax.axis_size(axis)
-    pairs = [(i, i + 2) for i in range(0, count - 2, 2)] + [(i, i - 2) for i in range(3, count, 2)]
-    return lax.ppermute(block, axis, pairs)
-
-
 def near_index(axis, size, inner=0):
     return jnp.where(lax.axis_index(axis) % 2 == 0, size - 1 - inner, inner)
 
@@ -61,7 +55,7 @@
     ref[(*index, slice(0, rows), slice(None))] = value
 
 
-def newton(n, y_ref, st_ref, r1_ref, kind_ref, count, w1_ref, w2_ref, nclass):
+def newton(n, y_ref, st_ref, r1_ref, kind_ref, counts, w1_ref, w2_ref, nclass):
     sp, nz = y_ref.shape[1:]
     deep = w1_ref.shape[0]
     tiles = [list(range(i, min(i + 2, n))) for i in range(0, n, 2)]
@@ -72,6 +66,7 @@
     def tall(value):
         return jnp.concatenate([value] * (sp // SUB), axis=0)
 
+    count = [counts[0, c] for c in range(nclass)]
     for low in range(nclass):
         live = nclass - low
 
@@ -114,12 +109,12 @@
     return total
 
 
-def start_row(i, target, cls, rate, y_ref, st_ref, r1_ref, kind_ref, nclass):
+def start_row(i, target, cls, inverse, y_ref, st_ref, r1_ref, kind_ref, nclass):
     sp, nz = target.shape
     kind = jnp.broadcast_to(cls, (SUB, nz))
-    inv = jnp.full((SUB, nz), 1.0 / rate[0], F32)
+    inv = inverse[0]
     for c in range(1, nclass):
-        inv = jnp.where(kind == c, 1.0 / rate[c], inv)
+        inv = jnp.where(kind == c, inverse[c], inv)
     y_ref[i] = target
     st_ref[i] = target * jnp.concatenate([inv] * (sp // SUB), axis=0)
     r1_ref[i] = inv + 1.0
@@ -131,17 +126,16 @@
     return jnp.where(me % 2 == 0, me > 0, me < last)
 
 
-def faces_kernel(nx, ny, ns, rate, count, dif, block, cls, mixing, fa, fy):
+def faces_kernel(nx, ny, ns, block, cls, fa, fya, fyb):
     xa, far = near_index("gx", nx), far_index("gx", nx)
+    for face, index in ((fyb, far_index), (fya, near_index)):
+        y, inner = index("gy", ny), index("gy", ny, 1)
+        for x in range(nx):
+            put(face, (x,), block[pl.ds(x * ny + y, ns, stride=nx * ny), :], ns)
+        put(face, (nx,), block[pl.ds(far * ny + inner, ns, stride=nx * ny), :], ns)
+        face[nx, ns : ns + 1, :] = cls[far, pl.ds(y, 1), :]
     for s in range(ns):
         fa[pl.ds(s * ny, ny), :] = block[pl.ds(s * nx * ny + xa * ny, ny), :]
-    for k, index in enumerate((near_index, far_index)):
-        y, inner = index("gy", ny), index("gy", ny, 1)
-        first = k * (nx + 1)
-        for x in range(nx):
-            put(fy, (first + x,), block[pl.ds(x * ny + y, ns, stride=nx * ny), :], ns)
-        put(fy, (first + nx,), block[pl.ds(far * ny + inner, ns, stride=nx * ny), :], ns)
-        fy[first + nx, ns : ns + 1, :] = cls[far, pl.ds(y, 1), :].astype(F32)
 
 
 def make_scale(scale, dif, ns):
@@ -174,8 +168,14 @@
     w2[:, 2 * deep :] = widen(jnp.concatenate(lows, axis=0), whole).astype(BF16)[:, :deep]
 
 
-def prep_kernel(nx, ny, ns, nclass, rate, dif, block, mixing, inverses, s_ref, scale, w1, w2, square):
+def prep_kernel(nx, ny, ns, nclass, rate, count, dif, block, mixing, inverses, s_ref, scale, w1, w2, inverse, counts, square):
     make_scale(scale, dif, ns)
+    lane = lax.broadcasted_iota(jnp.int32, counts.shape, 1)
+    found = jnp.zeros(counts.shape, jnp.int32)
+    for c in range(nclass):
+        inverse[c] = jnp.full(inverse.shape[1:], 1.0 / rate[c], F32)
+        found = jnp.where(lane == c, count[c], found)
+    counts[...] = found
     make_weights(w1, w2, square, mixing, inverses, rate, ns, s_ref.shape[2], nclass)
     for x in range(nx):
         for y in range(ny):
@@ -199,13 +199,13 @@
         part = v + scale[...] * lap(v, [s_ref[inner, y], low, high])
         message[pl.ds(ns * ny + y, ns, stride=ny), :] = part[:ns]
     base = 2 * ns * ny
-    message[pl.ds(base, ny), :] = cls[far].astype(F32)
+    message[pl.ds(base, ny), :] = cls[far]
     message[pl.ds(base + ny, ns, stride=2), :] = ya[far][:ns]
     message[pl.ds(base + ny + 1, ns, stride=2), :] = yb[far][:ns]
 
 
-def near_kernel(nx, ny, ns, nclass, rate, count, s_ref, halo, ya, yb, cls, scale, w1, w2,
-                f_ref, sec, face, fy, y_ref, st_ref, r1_ref, kind_ref):
+def near_kernel(nx, ny, ns, nclass, inverse, counts, s_ref, halo, ya, yb, cls, scale, w1, w2,
+                f_ref, sec, face, fya, fyb, y_ref, st_ref, r1_ref, kind_ref):
     sp, nz = s_ref.shape[2:]
     edge = edge_rows(ya, yb)
     near, inner, far = near_index("gx", nx), near_index("gx", nx, 1), far_index("gx", nx)
@@ -220,20 +220,20 @@
         v = s_ref[x, y]
         force = scale[...] * lap(v, nbrs)
         f_ref[x, y] = force
-        start_row(i, v + force, cls[x, y : y + 1, :], rate, y_ref, st_ref, r1_ref, kind_ref, nclass)
-    newton(len(places), y_ref, st_ref, r1_ref, kind_ref, count, w1, w2, nclass)
+        start_row(i, v + force, cls[x, y : y + 1, :], inverse, y_ref, st_ref, r1_ref, kind_ref, nclass)
+    newton(len(places), y_ref, st_ref, r1_ref, kind_ref, counts, w1, w2, nclass)
     for i, (x, y) in enumerate(places):
         sec[x, y] = y_ref[i]
         if i < ny:
             face[pl.ds(y, ns, stride=ny), :] = y_ref[i][:ns]
-    for k, y in enumerate((near_index("gy", ny), far_index("gy", ny))):
-        fy[k * nx + far] = jnp.zeros((sp, nz), F32)
-        fy[k * nx + near] = sec[near, y]
+    for fy, y in ((fya, near_index("gy", ny)), (fyb, far_index("gy", ny))):
+        fy[far] = jnp.zeros((sp, nz), F32)
+        fy[near] = sec[near, y]
         for x in range(1, nx - 1):
-            fy[k * nx + x] = sec[x, y]
-
-
-def far_kernel(nx, ny, ns, nclass, rate, count, s_ref, message, ya, yb, cls, scale, w1, w2, f_in, sec_in,
+            fy[x] = sec[x, y]
+
+
+def far_kernel(nx, ny, ns, nclass, inverse, counts, s_ref, message, ya, yb, cls, scale, w1, w2, f_in, sec_in,
                f_ref, sec, beyond, beside, y_ref, st_ref, r1_ref, kind_ref):
     sp = s_ref.shape[2]
     edge = edge_rows(ya, yb)
@@ -241,7 +241,7 @@
     base = 2 * ns * ny
 
     def begin(i, target, kind):
-        start_row(i, target, kind, rate, y_ref, st_ref, r1_ref, kind_ref, nclass)
+        start_row(i, target, kind, inverse, y_ref, st_ref, r1_ref, kind_ref, nclass)
 
     for y in range(ny):
         v = s_ref[far, y]
@@ -255,13 +255,13 @@
         f_ref[far, y] = force
         begin(y, v + force, cls[far, y : y + 1, :])
         target = widen(message[pl.ds(ns * ny + y, ns, stride=ny), :], sp) + scale[...] * v
-        begin(ny + y, target, message[pl.ds(base + y, 1), :].astype(jnp.int32))
+        begin(ny + y, target, message[pl.ds(base + y, 1), :])
     for k, (halo, y) in enumerate(((ya, near_index("gy", ny)), (yb, far_index("gy", ny)))):
         v = halo[far]
         corner = widen(message[pl.ds(base + ny + k, ns, stride=2), :], sp)
         target = v + scale[...] * lap(v, [halo[inner], corner, halo[nx], s_ref[far, y]])
-        begin(2 * ny + k, target, halo[nx, ns : ns + 1, :].astype(jnp.int32))
-    newton(2 * ny + 2, y_ref, st_ref, r1_ref, kind_ref, count, w1, w2, nclass)
+        begin(2 * ny + k, target, halo[nx, ns : ns + 1, :])
+    newton(2 * ny + 2, y_ref, st_ref, r1_ref, kind_ref, counts, w1, w2, nclass)
     there = exists("gx")
     for y in range(ny):
         sec[far, y] = y_ref[y]
@@ -329,53 +329,61 @@
             pltpu.VMEM((n, sp, nz), F32),
             pltpu.VMEM((n, sp, nz), F32),
             pltpu.VMEM((n, SUB, nz), F32),
-            pltpu.VMEM((n, SUB, nz), jnp.int32),
+            pltpu.VMEM((n, SUB, nz), F32),
         ]
 
     us = 10**9
     part = functools.partial
     rate, count = class_rate, newton_counts
-    fa, fy = call(
+    classes = cell_class.astype(F32)
+    fa, fya, fyb = call(
         part(faces_kernel, nx, ny, ns),
+        [],
+        [block, classes],
+        [xface, shape(nx + 1, sp, nz), shape(nx + 1, sp, nz)],
+    )
+    hyb = swap(fyb, "gy", 1)
+    ha = swap(fa, "gx", 0)
+    hya = swap(fya, "gy", 0)
+    s_ref, scale, w1, w2, inverse, counts = call(
+        part(prep_kernel, nx, ny, ns, nclass),
         [rate, count, diffusion],
-        [block, cell_class, mixing],
-        [xface, shape(2 * (nx + 1), sp, nz)],
-    )
-    hya = swap(fy, "gy", 0)
-    ha = swap(fa, "gx", 0)
-    hyb = hand_on(hya[nx + 1 :], "gy")
-    s_ref, scale, w1, w2 = call(
-        part(prep_kernel, nx, ny, ns, nclass),
-        [rate, diffusion],
         [block, mixing, inverses],
-        [field, shape(sp, nz), shape(deep, 3 * deep, dtype=BF16), shape(up(nclass * sp, 16), 3 * deep, dtype=BF16)],
+        [
+            field,
+            shape(sp, nz),
+            shape(deep, 3 * deep, dtype=BF16),
+            shape(up(nclass * sp, 16), 3 * deep, dtype=BF16),
+            shape(nclass, SUB, nz),
+            shape(SUB, nz, dtype=jnp.int32),
+        ],
         [pltpu.VMEM((deep, 2 * deep), F32)],
         work=us,
     )
     (message,) = call(
         part(send_kernel, nx, ny, ns),
         [],
-        [block, s_ref, hya, hyb, cell_class, scale],
+        [block, s_ref, hya, hyb, classes, scale],
         [shape(2 * ns * ny + ny + 2 * ns, nz)],
         work=us // 2,
     )
     message = swap(message, "gx", 1)
-    force, sec, fa, fy = call(
+    force, sec, fa, fya, fyb = call(
         part(near_kernel, nx, ny, ns, nclass),
-        [rate, count],
-        [s_ref, ha, hya, hyb, cell_class, scale, w1, w2],
-        [field, field, xface, shape(2 * nx, sp, nz)],
+        [],
+        [inverse, counts, s_ref, ha, hya, hyb, classes, scale, w1, w2],
+        [field, field, xface, shape(nx, sp, nz), shape(nx, sp, nz)],
         scratch((nx - 1) * ny),
         mib=14,
         work=6 * us,
     )
-    back_ya = swap(fy, "gy", 0)
+    back_ya = swap(fya, "gy", 0)
     ha = swap(fa, "gx", 0)
-    back_yb = hand_on(back_ya[nx:], "gy")
+    back_yb = swap(fyb, "gy", 1)
     force, sec, beyond, beside = call(
         part(far_kernel, nx, ny, ns, nclass),
-        [rate, count],
-        [s_ref, message, hya, hyb, cell_class, scale, w1, w2, force, sec],
+        [],
+        [inverse, counts, s_ref, message, hya, hyb, classes, scale, w1, w2, force, sec],
         [field, field, shape(ny, sp, nz), shape(2, sp, nz)],
         scratch(2 * ny + 2),
         mib=12,

time: 37 us -> 32.6 us (0.88)
  the two profiles are of different devices: /device:TPU:0 before, /device:TPU:1 now
where the time goes in v3:
time: 32.6 us; the launch traced here: 32.3 us
  Pallas kernels  14.1 us (43%)
  starting transfers between devices  14.1 us (43%)
  local copies, waits for them, and re-layouts  2.09 us (6%)
  waiting for transfers between devices  1.2 us (4%)
  other arithmetic  0.72 us (2%)
    pallas_call x6, Pallas kernels, call(): pl.pallas_call(kernel, out_shape=tuple(outs), in_specs=[SMEM] * len(small...  14.1 us
    ppermute x7, starting transfers between devices, swap(): return lax.ppermute(block, axis, pairs)  14.1 us
    unnamed x13, local copies, waits for them, and re-layouts  2.09 us
    ppermute x7, waiting for transfers between devices, swap(): return lax.ppermute(block, axis, pairs)  1.2 us
    convert_element_type x1, other arithmetic, local(): classes = cell_class.astype(F32)  0.72 us
  transfers between devices with their start and end apart: 7, of which 1 were waited for; matrix products, arithmetic and copies ran while one was open for 3% of the time, Pallas kernels for 36%

profile of v3, /device:TPU:1, one launch (start us, length us, event | category | flops | bytes accessed | tf_op | source)
XLA Modules:
  0.0 32.3 jit_solution(18345519469426313573)
XLA Ops:
  0.0 0.7 %convert_element_type.3.cls = f32[4,8,128]{2,1,0:T(8,128)S(1)} convert(s32[4,8,128]{2,1,0:T(8,128)} %param.13) | non-fusion elementwise | flops 4096 | bytes 32768 | tf_op jit(solution)/shard_map/convert_element_type | solution.py:338
  0.7 0.0 copy-start
  0.7 1.2 %copy-done = f32[53,4,8,128]{3,2,1,0:T(8,128)S(1)} copy-done((f32[53,4,8,128]{3,2,1,0:T(8,128)S(1)}, f32[53,4,8,128]{3,2,1,0:T(8,128)}, u32[]{:S(2)}) %copy-start) | copy-done | bytes 868376
  1.9 0.0 copy-start.1
  1.9 0.2 shard_map.74
  2.1 2.1 %collective-permute-start.3 = (f32[424,128]{1,0:T(8,128)S(1)}, f32[424,128]{1,0:T(8,128)S(1)}, u32[]{:S(2)}, u32[]{:S(2)}) collective-permute-start(f32[424,128]{1,0:T(8,128)S(1)} %get-tuple-element.31), channel_id=1, source_target_pairs={{0,4},{4,0},{8,12},{12,8},{16,20},{20,16},{24,28},{28,24},{1,5},{5... | collective-permute-start | bytes 651272 | tf_op jit(solution)/shard_map/ppermute | solution.py:27
  4.2 1.0 %collective-permute-start = (f32[5,56,128]{2,1,0:T(8,128)S(1)}, f32[5,56,128]{2,1,0:T(8,128)S(1)}, u32[]{:S(2)}, u32[]{:S(2)}) collective-permute-start(f32[5,56,128]{2,1,0:T(8,128)S(1)} %get-tuple-element.26), channel_id=1, source_target_pairs={{0,1},{1,0},{2,3},{3,2},{4,5},{5,4},{6,7},{7,6},{8,9},{9,8},{10,11... | collective-permute-start | bytes 430088 | tf_op jit(solution)/shard_map/ppermute | solution.py:27
  5.2 0.0 copy-start.2
  5.2 0.0 copy-start.3
  5.2 0.0 copy-start.4
  5.2 0.0 copy-start.5
  5.2 3.2 %collective-permute-start.1 = (f32[5,56,128]{2,1,0:T(8,128)S(1)}, f32[5,56,128]{2,1,0:T(8,128)S(1)}, u32[]{:S(2)}, u32[]{:S(2)}) collective-permute-start(f32[5,56,128]{2,1,0:T(8,128)S(1)} %get-tuple-element.27), channel_id=1, source_target_pairs={{1,2},{2,1},{5,6},{6,5},{9,10},{10,9},{13,14},{14,13},{17,18},{18,... | collective-permute-start | bytes 430088 | tf_op jit(solution)/shard_map/ppermute | solution.py:27
  8.3 0.9 %copy.10.inverses = f32[4,53,53]{2,1,0:T(8,128)S(1)} copy(f32[4,53,53]{2,0,1:T(4,128)} %param.11) | data formatting | bytes 89888 | tf_op args[4]
  9.3 0.0 copy-done.1
  9.3 0.0 copy-done.2
  9.3 0.0 copy-done.3
  9.3 0.0 copy-done.4
  9.3 0.0 copy-done.5
  9.3 1.2 %shard_map.73 = (f32[4,8,56,128]{3,2,1,0:T(8,128)S(1)}, f32[56,128]{1,0:T(8,128)S(1)}, bf16[64,192]{1,0:T(8,128)(2,1)S(1)}, bf16[224,192]{1,0:T(8,128)(2,1)S(1)}...) custom-call(f32[4]{0:T(128)S(1)} %copy-done.3, s32[4]{0:T(128)S(1)} %copy-done.4, f32[53]{0:T(128)S(1)} %copy-done.5, ...), custom_call_target="tpu_custom_call" | custom-call | flops 1000000000 | bytes 1 | tf_op jit(solution)/shard_map/pallas_call | solution.py:316
  10.5 0.0 collective-permute-done.ya
  10.5 1.2 %collective-permute-done.1.yb = f32[5,56,128]{2,1,0:T(8,128)S(1)} collective-permute-done((f32[5,56,128]{2,1,0:T(8,128)S(1)}, f32[5,56,128]{2,1,0:T(8,128)S(1)}, u32[]{:S(2)}, u32[]{:S(2)}) %collective-permute-start.1) | collective-permute-done | bytes 143392 | tf_op jit(solution)/shard_map/ppermute | solution.py:27
  11.7 0.2 shard_map.75
  11.9 0.7 %collective-permute-start.2 = (f32[962,128]{1,0:T(8,128)S(1)}, f32[962,128]{1,0:T(8,128)S(1)}, u32[]{:S(2)}, u32[]{:S(2)}) collective-permute-start(f32[962,128]{1,0:T(8,128)S(1)} %shard_map.75), channel_id=1, source_target_pairs={{4,8},{8,4},{12,16},{16,12},{20,24},{24,20},{5,9},{9,5},{13,17},{1... | collective-permute-start | bytes 1477640 | tf_op jit(solution)/shard_map/ppermute | solution.py:27
  12.6 0.0 collective-permute-done.3.halo
  12.7 5.6 %shard_map.76 = (f32[4,8,56,128]{3,2,1,0:T(8,128)S(1)}, f32[4,8,56,128]{3,2,1,0:T(8,128)S(1)}, f32[424,128]{1,0:T(8,128)S(1)}, f32[4,56,128]{2,1,0:T(8,128)S(1)}, f32[4,56,128]{2,1,0:T(8,128)S(1)}) custom-call(f32[4,8,128]{2,1,0:T(8,128)S(1)} %get-tuple-element.23.inverse, s32[8,128]{1,0:T(8,128)S(1)} %get-tuple-element.24.counts, ...), custom_call_target="tpu_custom_call" | custom-call | flops 6000000000 | bytes 1 | tf_op jit(solution)/shard_map/pallas_call | solution.py:316
  18.2 0.1 collective-permute-start.5
  18.3 3.0 %collective-permute-start.6 = (f32[4,56,128]{2,1,0:T(8,128)S(1)}, f32[4,56,128]{2,1,0:T(8,128)S(1)}, u32[]{:S(2)}, u32[]{:S(2)}) collective-permute-start(f32[4,56,128]{2,1,0:T(8,128)S(1)} %get-tuple-element.39), channel_id=1, source_target_pairs={{1,2},{2,1},{5,6},{6,5},{9,10},{10,9},{13,14},{14,13},{17,18},{18,... | collective-permute-start | bytes 344072 | tf_op jit(solution)/shard_map/ppermute | solution.py:27
  21.4 4.0 %collective-permute-start.4 = (f32[424,128]{1,0:T(8,128)S(1)}, f32[424,128]{1,0:T(8,128)S(1)}, u32[]{:S(2)}, u32[]{:S(2)}) collective-permute-start(f32[424,128]{1,0:T(8,128)S(1)} %get-tuple-element.36), channel_id=1, source_target_pairs={{0,4},{4,0},{8,12},{12,8},{16,20},{20,16},{24,28},{28,24},{1,5},{5... | collective-permute-start | bytes 651272 | tf_op jit(solution)/shard_map/ppermute | solution.py:27
  25.4 0.0 collective-permute-done.2.message
  25.4 4.6 %shard_map.77 = (f32[4,8,56,128]{3,2,1,0:T(8,128)S(1)}, f32[4,8,56,128]{3,2,1,0:T(8,128)S(1)}, f32[8,56,128]{2,1,0:T(8,128)S(1)}, f32[2,56,128]{2,1,0:T(8,128)S(1)}) custom-call(f32[4,8,128]{2,1,0:T(8,128)S(1)} %get-tuple-element.23.inverse, s32[8,128]{1,0:T(8,128)S(1)} %get-tuple-element.24.counts, ...), custom_call_target="tpu_custom_call", output_to_operand_aliasing={{0}: (10, {}), {1}: (11, {})} | custom-call | flops 5000000000 | bytes 1 | tf_op jit(solution)/shard_map/pallas_call | solution.py:316
  30.1 0.0 collective-permute-done.5.ya
  30.1 0.0 collective-permute-done.6.yb
  30.1 0.0 collective-permute-done.4.xa
  30.1 2.2 %shard_map.78 = f32[1696,128]{1,0:T(8,128)} custom-call(f32[4,8,56,128]{3,2,1,0:T(8,128)S(1)} %get-tuple-element.34.sec, f32[4,8,56,128]{3,2,1,0:T(8,128)S(1)} %get-tuple-element.35.f_ref, f32[424,128]{1,0:T(8,128)S(1)} %collective-permute-done.4.xa, f32[8,56,128]{2,1,0:T(8,128)S(1)} %get-tuple-element.37.beyond, ...), custom_call_target="tpu_custom_call" | custom-call | flops 2000000000 | bytes 1 | tf_op jit(solution)/shard_map/pallas_call | solution.py:316
Async XLA Ops:
  0.7 1.2 %copy-start = (f32[53,4,8,128]{3,2,1,0:T(8,128)S(1)}, f32[53,4,8,128]{3,2,1,0:T(8,128)}, u32[]{:S(2)}) copy-start(f32[53,4,8,128]{3,2,1,0:T(8,128)} %param.7) | copy-start | bytes 2605060
  1.9 7.4 %copy-start.1 = (f32[53,4,8,128]{3,2,1,0:T(8,128)S(1)}, f32[53,4,8,128]{3,2,1,0:T(8,128)}, u32[]{:S(2)}) copy-start(f32[53,4,8,128]{3,2,1,0:T(8,128)} %param.7) | copy-start | bytes 2605060
  2.1 10.5 %collective-permute-start.3 = (f32[424,128]{1,0:T(8,128)S(1)}, f32[424,128]{1,0:T(8,128)S(1)}, u32[]{:S(2)}, u32[]{:S(2)}) collective-permute-start(f32[424,128]{1,0:T(8,128)S(1)} %get-tuple-element.31), channel_id=1, source_target_pairs={{0,4},{4,0},{8,12},{12,8},{16,20},{20,16},{24,28},{28,24},{1,5},{5... | collective-permute-start | bytes 651272 | tf_op jit(solution)/shard_map/ppermute | solution.py:27
  4.2 6.3 %collective-permute-start = (f32[5,56,128]{2,1,0:T(8,128)S(1)}, f32[5,56,128]{2,1,0:T(8,128)S(1)}, u32[]{:S(2)}, u32[]{:S(2)}) collective-permute-start(f32[5,56,128]{2,1,0:T(8,128)S(1)} %get-tuple-element.26), channel_id=1, source_target_pairs={{0,1},{1,0},{2,3},{3,2},{4,5},{5,4},{6,7},{7,6},{8,9},{9,8},{10,11... | collective-permute-start | bytes 430088 | tf_op jit(solution)/shard_map/ppermute | solution.py:27
  5.2 4.1 %copy-start.2 = (f32[53,53]{1,0:T(8,128)S(1)}, f32[53,53]{1,0:T(8,128)}, u32[]{:S(2)}) copy-start(f32[53,53]{1,0:T(8,128)} %mixing.1) | copy-start | bytes 33712
  5.2 4.1 %copy-start.3 = (f32[4]{0:T(128)S(1)}, f32[4]{0:T(128)}, u32[]{:S(2)}) copy-start(f32[4]{0:T(128)} %rate.1) | copy-start | bytes 52
  5.2 4.1 %copy-start.4 = (s32[4]{0:T(128)S(1)}, s32[4]{0:T(128)}, u32[]{:S(2)}) copy-start(s32[4]{0:T(128)} %count.1) | copy-start | bytes 52
  5.2 4.1 %copy-start.5 = (f32[53]{0:T(128)S(1)}, f32[53]{0:T(128)}, u32[]{:S(2)}) copy-start(f32[53]{0:T(128)} %dif.1) | copy-start | bytes 640
  5.2 6.5 %collective-permute-start.1 = (f32[5,56,128]{2,1,0:T(8,128)S(1)}, f32[5,56,128]{2,1,0:T(8,128)S(1)}, u32[]{:S(2)}, u32[]{:S(2)}) collective-permute-start(f32[5,56,128]{2,1,0:T(8,128)S(1)} %get-tuple-element.27), channel_id=1, source_target_pairs={{1,2},{2,1},{5,6},{6,5},{9,10},{10,9},{13,14},{14,13},{17,18},{18,... | collective-permute-start | bytes 430088 | tf_op jit(solution)/shard_map/ppermute | solution.py:27
  11.9 13.5 %collective-permute-start.2 = (f32[962,128]{1,0:T(8,128)S(1)}, f32[962,128]{1,0:T(8,128)S(1)}, u32[]{:S(2)}, u32[]{:S(2)}) collective-permute-start(f32[962,128]{1,0:T(8,128)S(1)} %shard_map.75), channel_id=1, source_target_pairs={{4,8},{8,4},{12,16},{16,12},{20,24},{24,20},{5,9},{9,5},{13,17},{1... | collective-permute-start | bytes 1477640 | tf_op jit(solution)/shard_map/ppermute | solution.py:27
  18.2 11.8 %collective-permute-start.5 = (f32[4,56,128]{2,1,0:T(8,128)S(1)}, f32[4,56,128]{2,1,0:T(8,128)S(1)}, u32[]{:S(2)}, u32[]{:S(2)}) collective-permute-start(f32[4,56,128]{2,1,0:T(8,128)S(1)} %get-tuple-element.38), channel_id=1, source_target_pairs={{0,1},{1,0},{2,3},{3,2},{4,5},{5,4},{6,7},{7,6},{8,9},{9,8},{10,11... | collective-permute-start | bytes 344072 | tf_op jit(solution)/shard_map/ppermute | solution.py:27
  18.3 11.7 %collective-permute-start.6 = (f32[4,56,128]{2,1,0:T(8,128)S(1)}, f32[4,56,128]{2,1,0:T(8,128)S(1)}, u32[]{:S(2)}, u32[]{:S(2)}) collective-permute-start(f32[4,56,128]{2,1,0:T(8,128)S(1)} %get-tuple-element.39), channel_id=1, source_target_pairs={{1,2},{2,1},{5,6},{6,5},{9,10},{10,9},{13,14},{14,13},{17,18},{18,... | collective-permute-start | bytes 344072 | tf_op jit(solution)/shard_map/ppermute | solution.py:27
  21.4 8.7 %collective-permute-start.4 = (f32[424,128]{1,0:T(8,128)S(1)}, f32[424,128]{1,0:T(8,128)S(1)}, u32[]{:S(2)}, u32[]{:S(2)}) collective-permute-start(f32[424,128]{1,0:T(8,128)S(1)} %get-tuple-element.36), channel_id=1, source_target_pairs={{0,4},{4,0},{8,12},{12,8},{16,20},{20,16},{24,28},{28,24},{1,5},{5... | collective-permute-start | bytes 651272 | tf_op jit(solution)/shard_map/ppermute | solution.py:27

commit v4 on v3

--- a/solution.py
+++ b/solution.py
@@ -270,7 +270,7 @@
     beside[1] = jnp.where(exists("gy"), y_ref[2 * ny + 1], 0.0)
 
 
-def last_kernel(nx, ny, ns, sec, f_ref, xa, beyond, ya, yb, beside, scale, out):
+def last_kernel(nx, ny, ns, sec, f_ref, xa, beyond, ya, yb, beside, scale, out, layers, sems):
     sp = sec.shape[2]
     even_x = lax.axis_index("gx") % 2 == 0
     even_y = lax.axis_index("gy") % 2 == 0
@@ -286,7 +286,9 @@
         side = jnp.where(even_y == high, beside[0], beside[1])
         return jnp.where(even_x == (x == 0), side, value)
 
+    copies = []
     for x in range(nx):
+        layer = layers.at[x].reshape(ns * ny, layers.shape[-1])
         for y in range(ny):
             v = sec[x, y]
             nbrs = [
@@ -296,7 +298,11 @@
                 sec[x, y + 1] if y < ny - 1 else edge(x, True),
             ]
             value = v + 0.5 * (scale[...] * lap(v, nbrs) - f_ref[x, y])
-            out[pl.ds(x * ny + y, ns, stride=nx * ny), :] = value[:ns]
+            layer[pl.ds(y, ns, stride=ny), :] = value[:ns]
+        copies.append(pltpu.make_async_copy(layers.at[x], out.at[:, x], sems.at[x]))
+        copies[-1].start()
+    for copy in copies:
+        copy.wait()
 
 
 def local(species, diffusion, class_rate, mixing, inverses, newton_counts, cell_class):
@@ -312,12 +318,12 @@
     field = shape(nx, ny, sp, nz)
     xface = shape(ns * ny, nz)
 
-    def call(kernel, small, big, outs, scratch=(), mib=6, work=1, alias=()):
+    def call(kernel, small, big, outs, scratch=(), mib=6, work=1, alias=(), place=VMEM):
         return pl.pallas_call(
             kernel,
             out_shape=tuple(outs),
             in_specs=[SMEM] * len(small) + [VMEM] * len(big),
-            out_specs=(VMEM,) * len(outs),
+            out_specs=(place,) * len(outs),
             scratch_shapes=list(scratch),
             input_output_aliases=dict(alias),
             compiler_params=pltpu.CompilerParams(vmem_limit_bytes=mib * 2**20),
@@ -394,10 +400,12 @@
         part(last_kernel, nx, ny, ns),
         [],
         [sec, force, ha, beyond, back_ya, back_yb, beside, scale],
-        [shape(*block.shape)],
+        [shape(ns, nx, ny, nz)],
+        [pltpu.VMEM((nx, ns, ny, nz), F32), pltpu.SemaphoreType.DMA((nx,))],
         work=2 * us,
-    )
-    return out.reshape(species.shape)
+        place=pl.BlockSpec(memory_space=pl.ANY),
+    )
+    return out
 
 
 def solution(mesh):

time: 32.6 us -> 31.8 us (0.975)
  Pallas kernels: 14.1 us -> 13.3 us
    pallas_call x6, Pallas kernels: 14.1 us -> 13.3 us  [call(): pl.pallas_call(kernel, out_shape=tuple(outs), in_specs=[SMEM] * len(small...]
  transfers between devices with their start and end apart: 7 -> 7, of which waited for: 1 -> 1; matrix products, arithmetic and copies ran while one was open for 3% -> 3% of each run, Pallas kernels for 36% -> 37%
where the time goes in v4:
time: 31.8 us; the launch traced here: 31.5 us
  starting transfers between devices  14.1 us (44%)
  Pallas kernels  13.3 us (42%)
  local copies, waits for them, and re-layouts  2.09 us (7%)
  waiting for transfers between devices  1.2 us (4%)
  other arithmetic  0.72 us (2%)
    ppermute x7, starting transfers between devices, swap(): return lax.ppermute(block, axis, pairs)  14.1 us
    pallas_call x6, Pallas kernels, call(): pl.pallas_call(kernel, out_shape=tuple(outs), in_specs=[SMEM] * len(small...  13.3 us
    unnamed x13, local copies, waits for them, and re-layouts  2.09 us
    ppermute x7, waiting for transfers between devices, swap(): return lax.ppermute(block, axis, pairs)  1.2 us
    convert_element_type x1, other arithmetic, local(): classes = cell_class.astype(F32)  0.72 us
  transfers between devices with their start and end apart: 7, of which 1 were waited for; matrix products, arithmetic and copies ran while one was open for 3% of the time, Pallas kernels for 37%

profile of v4, /device:TPU:1, one launch (start us, length us, event | category | flops | bytes accessed | tf_op | source)
XLA Modules:
  0.0 31.5 jit_solution(18413569879841901868)
XLA Ops:
  0.0 0.7 %convert_element_type.3.cls = f32[4,8,128]{2,1,0:T(8,128)S(1)} convert(s32[4,8,128]{2,1,0:T(8,128)} %param.13) | non-fusion elementwise | flops 4096 | bytes 32768 | tf_op jit(solution)/shard_map/convert_element_type | solution.py:344
  0.7 0.0 copy-start
  0.7 1.2 %copy-done = f32[53,4,8,128]{3,2,1,0:T(8,128)S(1)} copy-done((f32[53,4,8,128]{3,2,1,0:T(8,128)S(1)}, f32[53,4,8,128]{3,2,1,0:T(8,128)}, u32[]{:S(2)}) %copy-start) | copy-done | bytes 868376
  1.9 0.0 copy-start.1
  1.9 0.2 shard_map.74
  2.1 2.1 %collective-permute-start.3 = (f32[424,128]{1,0:T(8,128)S(1)}, f32[424,128]{1,0:T(8,128)S(1)}, u32[]{:S(2)}, u32[]{:S(2)}) collective-permute-start(f32[424,128]{1,0:T(8,128)S(1)} %get-tuple-element.31), channel_id=1, source_target_pairs={{0,4},{4,0},{8,12},{12,8},{16,20},{20,16},{24,28},{28,24},{1,5},{5... | collective-permute-start | bytes 651272 | tf_op jit(solution)/shard_map/ppermute | solution.py:27
  4.2 1.0 %collective-permute-start = (f32[5,56,128]{2,1,0:T(8,128)S(1)}, f32[5,56,128]{2,1,0:T(8,128)S(1)}, u32[]{:S(2)}, u32[]{:S(2)}) collective-permute-start(f32[5,56,128]{2,1,0:T(8,128)S(1)} %get-tuple-element.26), channel_id=1, source_target_pairs={{0,1},{1,0},{2,3},{3,2},{4,5},{5,4},{6,7},{7,6},{8,9},{9,8},{10,11... | collective-permute-start | bytes 430088 | tf_op jit(solution)/shard_map/ppermute | solution.py:27
  5.2 0.0 copy-start.2
  5.2 0.0 copy-start.3
  5.2 0.0 copy-start.4
  5.2 0.0 copy-start.5
  5.2 3.2 %collective-permute-start.1 = (f32[5,56,128]{2,1,0:T(8,128)S(1)}, f32[5,56,128]{2,1,0:T(8,128)S(1)}, u32[]{:S(2)}, u32[]{:S(2)}) collective-permute-start(f32[5,56,128]{2,1,0:T(8,128)S(1)} %get-tuple-element.27), channel_id=1, source_target_pairs={{1,2},{2,1},{5,6},{6,5},{9,10},{10,9},{13,14},{14,13},{17,18},{18,... | collective-permute-start | bytes 430088 | tf_op jit(solution)/shard_map/ppermute | solution.py:27
  8.3 0.9 %copy.10.inverses = f32[4,53,53]{2,1,0:T(8,128)S(1)} copy(f32[4,53,53]{2,0,1:T(4,128)} %param.11) | data formatting | bytes 89888 | tf_op args[4]
  9.3 0.0 copy-done.1
  9.3 0.0 copy-done.2
  9.3 0.0 copy-done.3
  9.3 0.0 copy-done.4
  9.3 0.0 copy-done.5
  9.3 1.2 %shard_map.73 = (f32[4,8,56,128]{3,2,1,0:T(8,128)S(1)}, f32[56,128]{1,0:T(8,128)S(1)}, bf16[64,192]{1,0:T(8,128)(2,1)S(1)}, bf16[224,192]{1,0:T(8,128)(2,1)S(1)}...) custom-call(f32[4]{0:T(128)S(1)} %copy-done.3, s32[4]{0:T(128)S(1)} %copy-done.4, f32[53]{0:T(128)S(1)} %copy-done.5, ...), custom_call_target="tpu_custom_call" | custom-call | flops 1000000000 | bytes 1 | tf_op jit(solution)/shard_map/pallas_call | solution.py:322
  10.5 0.0 collective-permute-done.ya
  10.5 1.2 %collective-permute-done.1.yb = f32[5,56,128]{2,1,0:T(8,128)S(1)} collective-permute-done((f32[5,56,128]{2,1,0:T(8,128)S(1)}, f32[5,56,128]{2,1,0:T(8,128)S(1)}, u32[]{:S(2)}, u32[]{:S(2)}) %collective-permute-start.1) | collective-permute-done | bytes 143392 | tf_op jit(solution)/shard_map/ppermute | solution.py:27
  11.7 0.2 shard_map.75
  11.9 0.7 %collective-permute-start.2 = (f32[962,128]{1,0:T(8,128)S(1)}, f32[962,128]{1,0:T(8,128)S(1)}, u32[]{:S(2)}, u32[]{:S(2)}) collective-permute-start(f32[962,128]{1,0:T(8,128)S(1)} %shard_map.75), channel_id=1, source_target_pairs={{4,8},{8,4},{12,16},{16,12},{20,24},{24,20},{5,9},{9,5},{13,17},{1... | collective-permute-start | bytes 1477640 | tf_op jit(solution)/shard_map/ppermute | solution.py:27
  12.6 0.0 collective-permute-done.3.halo
  12.7 5.6 %shard_map.76 = (f32[4,8,56,128]{3,2,1,0:T(8,128)S(1)}, f32[4,8,56,128]{3,2,1,0:T(8,128)S(1)}, f32[424,128]{1,0:T(8,128)S(1)}, f32[4,56,128]{2,1,0:T(8,128)S(1)}, f32[4,56,128]{2,1,0:T(8,128)S(1)}) custom-call(f32[4,8,128]{2,1,0:T(8,128)S(1)} %get-tuple-element.23.inverse, s32[8,128]{1,0:T(8,128)S(1)} %get-tuple-element.24.counts, ...), custom_call_target="tpu_custom_call" | custom-call | flops 6000000000 | bytes 1 | tf_op jit(solution)/shard_map/pallas_call | solution.py:322
  18.2 0.1 collective-permute-start.5
  18.3 3.0 %collective-permute-start.6 = (f32[4,56,128]{2,1,0:T(8,128)S(1)}, f32[4,56,128]{2,1,0:T(8,128)S(1)}, u32[]{:S(2)}, u32[]{:S(2)}) collective-permute-start(f32[4,56,128]{2,1,0:T(8,128)S(1)} %get-tuple-element.39), channel_id=1, source_target_pairs={{1,2},{2,1},{5,6},{6,5},{9,10},{10,9},{13,14},{14,13},{17,18},{18,... | collective-permute-start | bytes 344072 | tf_op jit(solution)/shard_map/ppermute | solution.py:27
  21.4 4.0 %collective-permute-start.4 = (f32[424,128]{1,0:T(8,128)S(1)}, f32[424,128]{1,0:T(8,128)S(1)}, u32[]{:S(2)}, u32[]{:S(2)}) collective-permute-start(f32[424,128]{1,0:T(8,128)S(1)} %get-tuple-element.36), channel_id=1, source_target_pairs={{0,4},{4,0},{8,12},{12,8},{16,20},{20,16},{24,28},{28,24},{1,5},{5... | collective-permute-start | bytes 651272 | tf_op jit(solution)/shard_map/ppermute | solution.py:27
  25.4 0.0 collective-permute-done.2.message
  25.4 4.6 %shard_map.77 = (f32[4,8,56,128]{3,2,1,0:T(8,128)S(1)}, f32[4,8,56,128]{3,2,1,0:T(8,128)S(1)}, f32[8,56,128]{2,1,0:T(8,128)S(1)}, f32[2,56,128]{2,1,0:T(8,128)S(1)}) custom-call(f32[4,8,128]{2,1,0:T(8,128)S(1)} %get-tuple-element.23.inverse, s32[8,128]{1,0:T(8,128)S(1)} %get-tuple-element.24.counts, ...), custom_call_target="tpu_custom_call", output_to_operand_aliasing={{0}: (10, {}), {1}: (11, {})} | custom-call | flops 5000000000 | bytes 1 | tf_op jit(solution)/shard_map/pallas_call | solution.py:322
  30.1 0.0 collective-permute-done.5.ya
  30.1 0.0 collective-permute-done.6.yb
  30.1 0.0 collective-permute-done.4.xa
  30.1 1.4 %shard_map.78 = f32[53,4,8,128]{3,2,1,0:T(8,128)} custom-call(f32[4,8,56,128]{3,2,1,0:T(8,128)S(1)} %get-tuple-element.34.sec, f32[4,8,56,128]{3,2,1,0:T(8,128)S(1)} %get-tuple-element.35.f_ref, f32[424,128]{1,0:T(8,128)S(1)} %collective-permute-done.4.xa, f32[8,56,128]{2,1,0:T(8,128)S(1)} %get-tuple-element.37.beyond, ...), custom_call_target="tpu_custom_call" | custom-call | flops 2000000000 | bytes 1 | tf_op jit(solution)/shard_map/pallas_call | solution.py:322
Async XLA Ops:
  0.7 1.2 %copy-start = (f32[53,4,8,128]{3,2,1,0:T(8,128)S(1)}, f32[53,4,8,128]{3,2,1,0:T(8,128)}, u32[]{:S(2)}) copy-start(f32[53,4,8,128]{3,2,1,0:T(8,128)} %param.7) | copy-start | bytes 2605060
  1.9 7.4 %copy-start.1 = (f32[53,4,8,128]{3,2,1,0:T(8,128)S(1)}, f32[53,4,8,128]{3,2,1,0:T(8,128)}, u32[]{:S(2)}) copy-start(f32[53,4,8,128]{3,2,1,0:T(8,128)} %param.7) | copy-start | bytes 2605060
  2.1 10.5 %collective-permute-start.3 = (f32[424,128]{1,0:T(8,128)S(1)}, f32[424,128]{1,0:T(8,128)S(1)}, u32[]{:S(2)}, u32[]{:S(2)}) collective-permute-start(f32[424,128]{1,0:T(8,128)S(1)} %get-tuple-element.31), channel_id=1, source_target_pairs={{0,4},{4,0},{8,12},{12,8},{16,20},{20,16},{24,28},{28,24},{1,5},{5... | collective-permute-start | bytes 651272 | tf_op jit(solution)/shard_map/ppermute | solution.py:27
  4.2 6.3 %collective-permute-start = (f32[5,56,128]{2,1,0:T(8,128)S(1)}, f32[5,56,128]{2,1,0:T(8,128)S(1)}, u32[]{:S(2)}, u32[]{:S(2)}) collective-permute-start(f32[5,56,128]{2,1,0:T(8,128)S(1)} %get-tuple-element.26), channel_id=1, source_target_pairs={{0,1},{1,0},{2,3},{3,2},{4,5},{5,4},{6,7},{7,6},{8,9},{9,8},{10,11... | collective-permute-start | bytes 430088 | tf_op jit(solution)/shard_map/ppermute | solution.py:27
  5.2 4.1 %copy-start.2 = (f32[53,53]{1,0:T(8,128)S(1)}, f32[53,53]{1,0:T(8,128)}, u32[]{:S(2)}) copy-start(f32[53,53]{1,0:T(8,128)} %mixing.1) | copy-start | bytes 33712
  5.2 4.1 %copy-start.3 = (f32[4]{0:T(128)S(1)}, f32[4]{0:T(128)}, u32[]{:S(2)}) copy-start(f32[4]{0:T(128)} %rate.1) | copy-start | bytes 52
  5.2 4.1 %copy-start.4 = (s32[4]{0:T(128)S(1)}, s32[4]{0:T(128)}, u32[]{:S(2)}) copy-start(s32[4]{0:T(128)} %count.1) | copy-start | bytes 52
  5.2 4.1 %copy-start.5 = (f32[53]{0:T(128)S(1)}, f32[53]{0:T(128)}, u32[]{:S(2)}) copy-start(f32[53]{0:T(128)} %dif.1) | copy-start | bytes 640
  5.2 6.5 %collective-permute-start.1 = (f32[5,56,128]{2,1,0:T(8,128)S(1)}, f32[5,56,128]{2,1,0:T(8,128)S(1)}, u32[]{:S(2)}, u32[]{:S(2)}) collective-permute-start(f32[5,56,128]{2,1,0:T(8,128)S(1)} %get-tuple-element.27), channel_id=1, source_target_pairs={{1,2},{2,1},{5,6},{6,5},{9,10},{10,9},{13,14},{14,13},{17,18},{18,... | collective-permute-start | bytes 430088 | tf_op jit(solution)/shard_map/ppermute | solution.py:27
  11.9 13.5 %collective-permute-start.2 = (f32[962,128]{1,0:T(8,128)S(1)}, f32[962,128]{1,0:T(8,128)S(1)}, u32[]{:S(2)}, u32[]{:S(2)}) collective-permute-start(f32[962,128]{1,0:T(8,128)S(1)} %shard_map.75), channel_id=1, source_target_pairs={{4,8},{8,4},{12,16},{16,12},{20,24},{24,20},{5,9},{9,5},{13,17},{1... | collective-permute-start | bytes 1477640 | tf_op jit(solution)/shard_map/ppermute | solution.py:27
  18.2 11.8 %collective-permute-start.5 = (f32[4,56,128]{2,1,0:T(8,128)S(1)}, f32[4,56,128]{2,1,0:T(8,128)S(1)}, u32[]{:S(2)}, u32[]{:S(2)}) collective-permute-start(f32[4,56,128]{2,1,0:T(8,128)S(1)} %get-tuple-element.38), channel_id=1, source_target_pairs={{0,1},{1,0},{2,3},{3,2},{4,5},{5,4},{6,7},{7,6},{8,9},{9,8},{10,11... | collective-permute-start | bytes 344072 | tf_op jit(solution)/shard_map/ppermute | solution.py:27
  18.3 11.7 %collective-permute-start.6 = (f32[4,56,128]{2,1,0:T(8,128)S(1)}, f32[4,56,128]{2,1,0:T(8,128)S(1)}, u32[]{:S(2)}, u32[]{:S(2)}) collective-permute-start(f32[4,56,128]{2,1,0:T(8,128)S(1)} %get-tuple-element.39), channel_id=1, source_target_pairs={{1,2},{2,1},{5,6},{6,5},{9,10},{10,9},{13,14},{14,13},{17,18},{18,... | collective-permute-start | bytes 344072 | tf_op jit(solution)/shard_map/ppermute | solution.py:27
  21.4 8.7 %collective-permute-start.4 = (f32[424,128]{1,0:T(8,128)S(1)}, f32[424,128]{1,0:T(8,128)S(1)}, u32[]{:S(2)}, u32[]{:S(2)}) collective-permute-start(f32[424,128]{1,0:T(8,128)S(1)} %get-tuple-element.36), channel_id=1, source_target_pairs={{0,4},{4,0},{8,12},{12,8},{16,20},{20,16},{24,28},{28,24},{1,5},{5... | collective-permute-start | bytes 651272 | tf_op jit(solution)/shard_map/ppermute | solution.py:27

commit v5 on v4

--- a/solution.py
+++ b/solution.py
@@ -148,7 +148,7 @@
         scale[g : g + SUB, :] = value
 
 
-def make_weights(w1, w2, square, mixing, inverses, rate, ns, sp, nclass):
+def make_weights(w1, w2, square, mixing, inverses, ns, sp, nclass):
     deep = square.shape[0]
     square[...] = jnp.zeros_like(square)
     square[:ns, :ns] = mixing[...]
@@ -157,8 +157,8 @@
     w1[:, : 2 * deep] = (back + pltpu.roll(back, deep, 1)).astype(BF16)
     w1[:, 2 * deep :] = (value - back).astype(BF16)[:, :deep]
     highs, lows = [], []
-    for c in reversed(range(nclass)):
-        square[:ns, :ns] = inverses[c] * rate[c]
+    for c in range(nclass):
+        square[:ns, :ns] = inverses[c]
         value = square[:sp, :]
         back = value.astype(BF16).astype(F32)
         highs.append(back + pltpu.roll(back, deep, 1))
@@ -168,15 +168,18 @@
     w2[:, 2 * deep :] = widen(jnp.concatenate(lows, axis=0), whole).astype(BF16)[:, :deep]
 
 
-def prep_kernel(nx, ny, ns, nclass, rate, count, dif, block, mixing, inverses, s_ref, scale, w1, w2, inverse, counts, square):
+def scale_kernel(ns, nclass, rate, count, dif, scale, rates, counts):
     make_scale(scale, dif, ns)
     lane = lax.broadcasted_iota(jnp.int32, counts.shape, 1)
     found = jnp.zeros(counts.shape, jnp.int32)
     for c in range(nclass):
-        inverse[c] = jnp.full(inverse.shape[1:], 1.0 / rate[c], F32)
+        rates[c] = jnp.full(rates.shape[1:], 1.0 / rate[c], F32)
         found = jnp.where(lane == c, count[c], found)
     counts[...] = found
-    make_weights(w1, w2, square, mixing, inverses, rate, ns, s_ref.shape[2], nclass)
+
+
+def prep_kernel(nx, ny, ns, nclass, block, mixing, inverses, s_ref, w1, w2, square):
+    make_weights(w1, w2, square, mixing, inverses, ns, s_ref.shape[2], nclass)
     for x in range(nx):
         for y in range(ny):
             put(s_ref, (x, y), block[pl.ds(x * ny + y, ns, stride=nx * ny), :], ns)
@@ -187,16 +190,19 @@
     return lambda x, high: jnp.where(even_y == high, ya[x], yb[x])
 
 
-def send_kernel(nx, ny, ns, block, s_ref, ya, yb, cls, scale, message):
+def send_kernel(nx, ny, ns, block, ya, yb, cls, scale, message, rows):
     far, inner = far_index("gx", nx), far_index("gx", nx, 1)
     edge = edge_rows(ya, yb)
     for s in range(ns):
         message[pl.ds(s * ny, ny), :] = block[pl.ds(s * nx * ny + far * ny, ny), :]
     for y in range(ny):
-        v = s_ref[far, y]
-        low = s_ref[far, y - 1] if y > 0 else edge(far, False)
-        high = s_ref[far, y + 1] if y < ny - 1 else edge(far, True)
-        part = v + scale[...] * lap(v, [s_ref[inner, y], low, high])
+        put(rows, (y,), message[pl.ds(y, ns, stride=ny), :], ns)
+    for y in range(ny):
+        v = rows[y]
+        low = rows[y - 1] if y > 0 else edge(far, False)
+        high = rows[y + 1] if y < ny - 1 else edge(far, True)
+        within = widen(block[pl.ds(inner * ny + y, ns, stride=nx * ny), :], rows.shape[1])
+        part = v + scale[...] * lap(v, [within, low, high])
         message[pl.ds(ns * ny + y, ns, stride=ny), :] = part[:ns]
     base = 2 * ns * ny
     message[pl.ds(base, ny), :] = cls[far]
@@ -351,29 +357,31 @@
     hyb = swap(fyb, "gy", 1)
     ha = swap(fa, "gx", 0)
     hya = swap(fya, "gy", 0)
-    s_ref, scale, w1, w2, inverse, counts = call(
+    scale, inverse, counts = call(
+        part(scale_kernel, ns, nclass),
+        [rate, count, diffusion],
+        [],
+        [shape(sp, nz), shape(nclass, SUB, nz), shape(SUB, nz, dtype=jnp.int32)],
+        work=us // 2,
+    )
+    (message,) = call(
+        part(send_kernel, nx, ny, ns),
+        [],
+        [block, hya, hyb, classes, scale],
+        [shape(2 * ns * ny + ny + 2 * ns, nz)],
+        [pltpu.VMEM((ny, sp, nz), F32)],
+        work=us // 2,
+    )
+    message = swap(message, "gx", 1)
+    scaled = (inverses * rate[:, None, None])[::-1]
+    s_ref, w1, w2 = call(
         part(prep_kernel, nx, ny, ns, nclass),
-        [rate, count, diffusion],
-        [block, mixing, inverses],
-        [
-            field,
-            shape(sp, nz),
-            shape(deep, 3 * deep, dtype=BF16),
-            shape(up(nclass * sp, 16), 3 * deep, dtype=BF16),
-            shape(nclass, SUB, nz),
-            shape(SUB, nz, dtype=jnp.int32),
-        ],
+        [],
+        [block, mixing, scaled],
+        [field, shape(deep, 3 * deep, dtype=BF16), shape(up(nclass * sp, 16), 3 * deep, dtype=BF16)],
         [pltpu.VMEM((deep, 2 * deep), F32)],
         work=us,
     )
-    (message,) = call(
-        part(send_kernel, nx, ny, ns),
-        [],
-        [block, s_ref, hya, hyb, classes, scale],
-        [shape(2 * ns * ny + ny + 2 * ns, nz)],
-        work=us // 2,
-    )
-    message = swap(message, "gx", 1)
     force, sec, fa, fya, fyb = call(
         part(near_kernel, nx, ny, ns, nclass),
         [],

time: 31.8 us -> 30.8 us (0.969)
  the two profiles are of different devices: /device:TPU:1 before, /device:TPU:9 now
where the time goes in v5:
time: 30.8 us; the launch traced here: 30.5 us
  Pallas kernels  13.2 us (43%)
  starting transfers between devices  12.8 us (42%)
  local copies, waits for them, and re-layouts  2.36 us (8%)
  waiting for transfers between devices  1.2 us (4%)
  other arithmetic  0.8 us (3%)
    pallas_call x7, Pallas kernels, call(): pl.pallas_call(kernel, out_shape=tuple(outs), in_specs=[SMEM] * len(small...  13.2 us
    ppermute x7, starting transfers between devices, swap(): return lax.ppermute(block, axis, pairs)  12.8 us
    unnamed x14, local copies, waits for them, and re-layouts  2.35 us
    ppermute x7, waiting for transfers between devices, swap(): return lax.ppermute(block, axis, pairs)  1.2 us
    convert_element_type x1, other arithmetic, local(): classes = cell_class.astype(F32)  0.72 us
  transfers between devices with their start and end apart: 7, of which 2 were waited for; matrix products, arithmetic and copies ran while one was open for 0% of the time, Pallas kernels for 38%

profile of v5, /device:TPU:9, one launch (start us, length us, event | category | flops | bytes accessed | tf_op | source)
XLA Modules:
  0.0 30.5 jit_solution(1442579608203023252)
XLA Ops:
  0.0 0.7 %convert_element_type.3.cls = f32[4,8,128]{2,1,0:T(8,128)S(1)} convert(s32[4,8,128]{2,1,0:T(8,128)} %param.13) | non-fusion elementwise | flops 4096 | bytes 32768 | tf_op jit(solution)/shard_map/convert_element_type | solution.py:350
  0.7 0.0 copy-start
  0.7 1.2 %copy-done = f32[53,4,8,128]{3,2,1,0:T(8,128)S(1)} copy-done((f32[53,4,8,128]{3,2,1,0:T(8,128)S(1)}, f32[53,4,8,128]{3,2,1,0:T(8,128)}, u32[]{:S(2)}) %copy-start) | copy-done | bytes 868376
  1.9 0.0 copy-start.6
  1.9 0.2 shard_map.75
  2.1 0.7 %collective-permute-start = (f32[5,56,128]{2,1,0:T(8,128)S(1)}, f32[5,56,128]{2,1,0:T(8,128)S(1)}, u32[]{:S(2)}, u32[]{:S(2)}) collective-permute-start(f32[5,56,128]{2,1,0:T(8,128)S(1)} %get-tuple-element.26), channel_id=1, source_target_pairs={{0,1},{1,0},{2,3},{3,2},{4,5},{5,4},{6,7},{7,6},{8,9},{9,8},{10,11... | collective-permute-start | bytes 430088 | tf_op jit(solution)/shard_map/ppermute | solution.py:27
  2.8 0.0 copy-start.2
  2.8 3.1 %collective-permute-start.1 = (f32[5,56,128]{2,1,0:T(8,128)S(1)}, f32[5,56,128]{2,1,0:T(8,128)S(1)}, u32[]{:S(2)}, u32[]{:S(2)}) collective-permute-start(f32[5,56,128]{2,1,0:T(8,128)S(1)} %get-tuple-element.27), channel_id=1, source_target_pairs={{1,2},{2,1},{5,6},{6,5},{9,10},{10,9},{13,14},{14,13},{17,18},{18,... | collective-permute-start | bytes 430088 | tf_op jit(solution)/shard_map/ppermute | solution.py:27
  5.9 1.3 %collective-permute-start.3 = (f32[424,128]{1,0:T(8,128)S(1)}, f32[424,128]{1,0:T(8,128)S(1)}, u32[]{:S(2)}, u32[]{:S(2)}) collective-permute-start(f32[424,128]{1,0:T(8,128)S(1)} %get-tuple-element.31), channel_id=1, source_target_pairs={{0,4},{4,0},{8,12},{12,8},{16,20},{20,16},{24,28},{28,24},{1,5},{5... | collective-permute-start | bytes 651272 | tf_op jit(solution)/shard_map/ppermute | solution.py:27
  7.2 0.0 copy-done.6
  7.2 0.0 copy-done.2
  7.2 0.1 copy_multiply_fusion
  7.3 0.0 copy-start.4
  7.3 0.0 copy-start.5
  7.3 0.6 %copy-done.4 = s32[4]{0:T(128)S(1)} copy-done((s32[4]{0:T(128)S(1)}, s32[4]{0:T(128)}, u32[]{:S(2)}) %copy-start.4) | copy-done | bytes 40
  7.9 0.0 copy-done.5
  7.9 0.0 copy-start.1
  7.9 0.0 copy-start.3
  7.9 0.6 %shard_map.73 = (f32[56,128]{1,0:T(8,128)S(1)}, f32[4,8,128]{2,1,0:T(8,128)S(1)}, s32[8,128]{1,0:T(8,128)S(1)}) custom-call(f32[4]{0:T(128)S(1)} %copy-done.2, s32[4]{0:T(128)S(1)} %copy-done.4, f32[53]{0:T(128)S(1)} %copy-done.5), custom_call_target="tpu_custom_call" | custom-call | flops 500000000 | bytes 1 | tf_op jit(solution)/shard_map/pallas_call | solution.py:328
  8.6 0.5 %copy-done.1 = f32[53,4,8,128]{3,2,1,0:T(8,128)S(1)} copy-done((f32[53,4,8,128]{3,2,1,0:T(8,128)S(1)}, f32[53,4,8,128]{3,2,1,0:T(8,128)}, u32[]{:S(2)}) %copy-start.1) | copy-done | bytes 868376
  9.1 0.0 copy-done.3
  9.1 0.6 %shard_map.74 = (f32[4,8,56,128]{3,2,1,0:T(8,128)S(1)}, bf16[64,192]{1,0:T(8,128)(2,1)S(1)}, bf16[224,192]{1,0:T(8,128)(2,1)S(1)}) custom-call(f32[1696,128]{1,0:T(8,128)S(1)} %bitcast.2, f32[53,53]{1,0:T(8,128)S(1)} %copy-done.3, f32[4,53,53]{2,1,0:T(8,128)S(1)} %rev.3.inverses), custom_call_target="tpu_custom_call" | custom-call | flops 1000000000 | bytes 1 | tf_op jit(solution)/shard_map/pallas_call | solution.py:328
  9.7 0.0 collective-permute-done.ya
  9.7 0.0 collective-permute-done.1.yb
  9.7 0.3 %shard_map.76 = f32[962,128]{1,0:T(8,128)S(1)} custom-call(f32[1696,128]{1,0:T(8,128)S(1)} %bitcast.3, f32[5,56,128]{2,1,0:T(8,128)S(1)} %collective-permute-done.ya, f32[5,56,128]{2,1,0:T(8,128)S(1)} %collective-permute-done.1.yb, f32[4,8,128]{2,1,0:T(8,128)S(1)} %convert_element_type.3.cls, f32[56,128]{1,0:T(8,128)S(1)} %get-tuple-element.28.scale), custom_call_target="tpu_custom_call" | custom-call | flops 500000000 | bytes 1 | tf_op jit(solution)/shard_map/pallas_call | solution.py:328
  10.0 2.8 %collective-permute-start.2 = (f32[962,128]{1,0:T(8,128)S(1)}, f32[962,128]{1,0:T(8,128)S(1)}, u32[]{:S(2)}, u32[]{:S(2)}) collective-permute-start(f32[962,128]{1,0:T(8,128)S(1)} %shard_map.76), channel_id=1, source_target_pairs={{4,8},{8,4},{12,16},{16,12},{20,24},{24,20},{5,9},{9,5},{13,17},{1... | collective-permute-start | bytes 1477640 | tf_op jit(solution)/shard_map/ppermute | solution.py:27
  12.9 0.0 collective-permute-done.3.halo
  12.9 5.5 %shard_map.77 = (f32[4,8,56,128]{3,2,1,0:T(8,128)S(1)}, f32[4,8,56,128]{3,2,1,0:T(8,128)S(1)}, f32[424,128]{1,0:T(8,128)S(1)}, f32[4,56,128]{2,1,0:T(8,128)S(1)}, f32[4,56,128]{2,1,0:T(8,128)S(1)}) custom-call(f32[4,8,128]{2,1,0:T(8,128)S(1)} %get-tuple-element.23.inverse, s32[8,128]{1,0:T(8,128)S(1)} %get-tuple-element.24.counts, ...), custom_call_target="tpu_custom_call" | custom-call | flops 6000000000 | bytes 1 | tf_op jit(solution)/shard_map/pallas_call | solution.py:328
  18.4 0.1 collective-permute-start.5
  18.5 3.1 %collective-permute-start.6 = (f32[4,56,128]{2,1,0:T(8,128)S(1)}, f32[4,56,128]{2,1,0:T(8,128)S(1)}, u32[]{:S(2)}, u32[]{:S(2)}) collective-permute-start(f32[4,56,128]{2,1,0:T(8,128)S(1)} %get-tuple-element.39), channel_id=1, source_target_pairs={{1,2},{2,1},{5,6},{6,5},{9,10},{10,9},{13,14},{14,13},{17,18},{18,... | collective-permute-start | bytes 344072 | tf_op jit(solution)/shard_map/ppermute | solution.py:27
  21.6 1.7 %collective-permute-start.4 = (f32[424,128]{1,0:T(8,128)S(1)}, f32[424,128]{1,0:T(8,128)S(1)}, u32[]{:S(2)}, u32[]{:S(2)}) collective-permute-start(f32[424,128]{1,0:T(8,128)S(1)} %get-tuple-element.36), channel_id=1, source_target_pairs={{0,4},{4,0},{8,12},{12,8},{16,20},{20,16},{24,28},{28,24},{1,5},{5... | collective-permute-start | bytes 651272 | tf_op jit(solution)/shard_map/ppermute | solution.py:27
  23.3 1.0 %collective-permute-done.2.message = f32[962,128]{1,0:T(8,128)S(1)} collective-permute-done((f32[962,128]{1,0:T(8,128)S(1)}, f32[962,128]{1,0:T(8,128)S(1)}, u32[]{:S(2)}, u32[]{:S(2)}) %collective-permute-start.2) | collective-permute-done | bytes 492576 | tf_op jit(solution)/shard_map/ppermute | solution.py:27
  24.3 4.6 %shard_map.78 = (f32[4,8,56,128]{3,2,1,0:T(8,128)S(1)}, f32[4,8,56,128]{3,2,1,0:T(8,128)S(1)}, f32[8,56,128]{2,1,0:T(8,128)S(1)}, f32[2,56,128]{2,1,0:T(8,128)S(1)}) custom-call(f32[4,8,128]{2,1,0:T(8,128)S(1)} %get-tuple-element.23.inverse, s32[8,128]{1,0:T(8,128)S(1)} %get-tuple-element.24.counts, ...), custom_call_target="tpu_custom_call", output_to_operand_aliasing={{0}: (10, {}), {1}: (11, {})} | custom-call | flops 5000000000 | bytes 1 | tf_op jit(solution)/shard_map/pallas_call | solution.py:328
  28.9 0.0 collective-permute-done.5.ya
  28.9 0.0 collective-permute-done.6.yb
  28.9 0.2 collective-permute-done.4.xa
  29.1 1.4 %shard_map.79 = f32[53,4,8,128]{3,2,1,0:T(8,128)} custom-call(f32[4,8,56,128]{3,2,1,0:T(8,128)S(1)} %get-tuple-element.34.sec, f32[4,8,56,128]{3,2,1,0:T(8,128)S(1)} %get-tuple-element.35.f_ref, f32[424,128]{1,0:T(8,128)S(1)} %collective-permute-done.4.xa, f32[8,56,128]{2,1,0:T(8,128)S(1)} %get-tuple-element.37.beyond, ...), custom_call_target="tpu_custom_call" | custom-call | flops 2000000000 | bytes 1 | tf_op jit(solution)/shard_map/pallas_call | solution.py:328
  (1 shorter events, 0.0 us)
Async XLA Ops:
  0.7 1.2 %copy-start = (f32[53,4,8,128]{3,2,1,0:T(8,128)S(1)}, f32[53,4,8,128]{3,2,1,0:T(8,128)}, u32[]{:S(2)}) copy-start(f32[53,4,8,128]{3,2,1,0:T(8,128)} %param.7) | copy-start | bytes 2605060
  1.9 5.3 %copy-start.6 = (f32[4,53,53]{2,0,1:T(4,128)S(1)}, f32[4,53,53]{2,0,1:T(4,128)}, u32[]{:S(2)}) copy-start(f32[4,53,53]{2,0,1:T(4,128)} %param.11) | copy-start | bytes 134836
  2.1 7.6 %collective-permute-start = (f32[5,56,128]{2,1,0:T(8,128)S(1)}, f32[5,56,128]{2,1,0:T(8,128)S(1)}, u32[]{:S(2)}, u32[]{:S(2)}) collective-permute-start(f32[5,56,128]{2,1,0:T(8,128)S(1)} %get-tuple-element.26), channel_id=1, source_target_pairs={{0,1},{1,0},{2,3},{3,2},{4,5},{5,4},{6,7},{7,6},{8,9},{9,8},{10,11... | collective-permute-start | bytes 430088 | tf_op jit(solution)/shard_map/ppermute | solution.py:27
  2.8 4.3 %copy-start.2 = (f32[4]{0:T(128)S(1)}, f32[4]{0:T(128)}, u32[]{:S(2)}) copy-start(f32[4]{0:T(128)} %rate.1) | copy-start | bytes 52
  2.8 6.8 %collective-permute-start.1 = (f32[5,56,128]{2,1,0:T(8,128)S(1)}, f32[5,56,128]{2,1,0:T(8,128)S(1)}, u32[]{:S(2)}, u32[]{:S(2)}) collective-permute-start(f32[5,56,128]{2,1,0:T(8,128)S(1)} %get-tuple-element.27), channel_id=1, source_target_pairs={{1,2},{2,1},{5,6},{6,5},{9,10},{10,9},{13,14},{14,13},{17,18},{18,... | collective-permute-start | bytes 430088 | tf_op jit(solution)/shard_map/ppermute | solution.py:27
  5.9 7.0 %collective-permute-start.3 = (f32[424,128]{1,0:T(8,128)S(1)}, f32[424,128]{1,0:T(8,128)S(1)}, u32[]{:S(2)}, u32[]{:S(2)}) collective-permute-start(f32[424,128]{1,0:T(8,128)S(1)} %get-tuple-element.31), channel_id=1, source_target_pairs={{0,4},{4,0},{8,12},{12,8},{16,20},{20,16},{24,28},{28,24},{1,5},{5... | collective-permute-start | bytes 651272 | tf_op jit(solution)/shard_map/ppermute | solution.py:27
  7.3 0.7 %copy-start.4 = (s32[4]{0:T(128)S(1)}, s32[4]{0:T(128)}, u32[]{:S(2)}) copy-start(s32[4]{0:T(128)} %count.1) | copy-start | bytes 52
  7.3 0.7 %copy-start.5 = (f32[53]{0:T(128)S(1)}, f32[53]{0:T(128)}, u32[]{:S(2)}) copy-start(f32[53]{0:T(128)} %dif.1) | copy-start | bytes 640
  7.9 1.2 %copy-start.1 = (f32[53,4,8,128]{3,2,1,0:T(8,128)S(1)}, f32[53,4,8,128]{3,2,1,0:T(8,128)}, u32[]{:S(2)}) copy-start(f32[53,4,8,128]{3,2,1,0:T(8,128)} %param.7) | copy-start | bytes 2605060
  7.9 1.2 %copy-start.3 = (f32[53,53]{1,0:T(8,128)S(1)}, f32[53,53]{1,0:T(8,128)}, u32[]{:S(2)}) copy-start(f32[53,53]{1,0:T(8,128)} %mixing.1) | copy-start | bytes 33712
  10.0 14.3 %collective-permute-start.2 = (f32[962,128]{1,0:T(8,128)S(1)}, f32[962,128]{1,0:T(8,128)S(1)}, u32[]{:S(2)}, u32[]{:S(2)}) collective-permute-start(f32[962,128]{1,0:T(8,128)S(1)} %shard_map.76), channel_id=1, source_target_pairs={{4,8},{8,4},{12,16},{16,12},{20,24},{24,20},{5,9},{9,5},{13,17},{1... | collective-permute-start | bytes 1477640 | tf_op jit(solution)/shard_map/ppermute | solution.py:27
  18.4 10.5 %collective-permute-start.5 = (f32[4,56,128]{2,1,0:T(8,128)S(1)}, f32[4,56,128]{2,1,0:T(8,128)S(1)}, u32[]{:S(2)}, u32[]{:S(2)}) collective-permute-start(f32[4,56,128]{2,1,0:T(8,128)S(1)} %get-tuple-element.38), channel_id=1, source_target_pairs={{0,1},{1,0},{2,3},{3,2},{4,5},{5,4},{6,7},{7,6},{8,9},{9,8},{10,11... | collective-permute-start | bytes 344072 | tf_op jit(solution)/shard_map/ppermute | solution.py:27
  18.5 10.4 %collective-permute-start.6 = (f32[4,56,128]{2,1,0:T(8,128)S(1)}, f32[4,56,128]{2,1,0:T(8,128)S(1)}, u32[]{:S(2)}, u32[]{:S(2)}) collective-permute-start(f32[4,56,128]{2,1,0:T(8,128)S(1)} %get-tuple-element.39), channel_id=1, source_target_pairs={{1,2},{2,1},{5,6},{6,5},{9,10},{10,9},{13,14},{14,13},{17,18},{18,... | collective-permute-start | bytes 344072 | tf_op jit(solution)/shard_map/ppermute | solution.py:27
  21.6 7.5 %collective-permute-start.4 = (f32[424,128]{1,0:T(8,128)S(1)}, f32[424,128]{1,0:T(8,128)S(1)}, u32[]{:S(2)}, u32[]{:S(2)}) collective-permute-start(f32[424,128]{1,0:T(8,128)S(1)} %get-tuple-element.36), channel_id=1, source_target_pairs={{0,4},{4,0},{8,12},{12,8},{16,20},{20,16},{24,28},{28,24},{1,5},{5... | collective-permute-start | bytes 651272 | tf_op jit(solution)/shard_map/ppermute | solution.py:27

commit v6 on v5

--- a/solution.py
+++ b/solution.py
@@ -58,7 +58,7 @@
 def newton(n, y_ref, st_ref, r1_ref, kind_ref, counts, w1_ref, w2_ref, nclass):
     sp, nz = y_ref.shape[1:]
     deep = w1_ref.shape[0]
-    tiles = [list(range(i, min(i + 2, n))) for i in range(0, n, 2)]
+    tiles = [list(range(i, min(i + 6, n))) for i in range(0, n, 6)]
 
     def lanes(ref, rows):
         return jnp.concatenate([ref[r] for r in rows], axis=1)
@@ -126,6 +126,10 @@
     return jnp.where(me % 2 == 0, me > 0, me < last)
 
 
+def classes_kernel(cell_class, classes):
+    classes[...] = cell_class[...].astype(F32)
+
+
 def faces_kernel(nx, ny, ns, block, cls, fa, fya, fyb):
     xa, far = near_index("gx", nx), far_index("gx", nx)
     for face, index in ((fyb, far_index), (fya, near_index)):
@@ -168,7 +172,8 @@
     w2[:, 2 * deep :] = widen(jnp.concatenate(lows, axis=0), whole).astype(BF16)[:, :deep]
 
 
-def scale_kernel(ns, nclass, rate, count, dif, scale, rates, counts):
+def scale_kernel(ns, nclass, rate, count, dif, mixing, scale, rates, counts, mixed):
+    mixed[...] = mixing[...]
     make_scale(scale, dif, ns)
     lane = lax.broadcasted_iota(jnp.int32, counts.shape, 1)
     found = jnp.zeros(counts.shape, jnp.int32)
@@ -347,7 +352,7 @@
     us = 10**9
     part = functools.partial
     rate, count = class_rate, newton_counts
-    classes = cell_class.astype(F32)
+    (classes,) = call(classes_kernel, [], [cell_class], [shape(nx, ny, nz)], work=8 * us)
     fa, fya, fyb = call(
         part(faces_kernel, nx, ny, ns),
         [],
@@ -357,11 +362,11 @@
     hyb = swap(fyb, "gy", 1)
     ha = swap(fa, "gx", 0)
     hya = swap(fya, "gy", 0)
-    scale, inverse, counts = call(
+    scale, inverse, counts, mixed = call(
         part(scale_kernel, ns, nclass),
         [rate, count, diffusion],
-        [],
-        [shape(sp, nz), shape(nclass, SUB, nz), shape(SUB, nz, dtype=jnp.int32)],
+        [mixing],
+        [shape(sp, nz), shape(nclass, SUB, nz), shape(SUB, nz, dtype=jnp.int32), shape(ns, ns)],
         work=us // 2,
     )
     (message,) = call(
@@ -377,7 +382,7 @@
     s_ref, w1, w2 = call(
         part(prep_kernel, nx, ny, ns, nclass),
         [],
-        [block, mixing, scaled],
+        [block, mixed, scaled],
         [field, shape(deep, 3 * deep, dtype=BF16), shape(up(nclass * sp, 16), 3 * deep, dtype=BF16)],
         [pltpu.VMEM((deep, 2 * deep), F32)],
         work=us,

time: 30.8 us -> 29.4 us (0.955)
  the two profiles are of different devices: /device:TPU:9 before, /device:TPU:25 now
where the time goes in v6:
time: 29.4 us; the launch traced here: 29.2 us
  Pallas kernels  13.2 us (45%)
  starting transfers between devices  11.3 us (38%)
  waiting for transfers between devices  2.53 us (9%)
  local copies, waits for them, and re-layouts  1.9 us (6%)
    pallas_call x8, Pallas kernels, call(): pl.pallas_call(kernel, out_shape=tuple(outs), in_specs=[SMEM] * len(small...  13.2 us
    ppermute x7, starting transfers between devices, swap(): return lax.ppermute(block, axis, pairs)  11.3 us
    ppermute x7, waiting for transfers between devices, swap(): return lax.ppermute(block, axis, pairs)  2.53 us
    unnamed x14, local copies, waits for them, and re-layouts  1.89 us
  transfers between devices with their start and end apart: 7, of which 2 were waited for; matrix products, arithmetic and copies ran while one was open for 0% of the time, Pallas kernels for 40%

profile of v6, /device:TPU:25, one launch (start us, length us, event | category | flops | bytes accessed | tf_op | source)
XLA Modules:
  0.0 29.2 jit_solution(279273979296963022)
XLA Ops:
  0.0 0.0 copy-start
  0.0 0.0 copy-start.3
  0.0 0.8 %copy-done.3 = s32[4,8,128]{2,1,0:T(8,128)S(1)} copy-done((s32[4,8,128]{2,1,0:T(8,128)S(1)}, s32[4,8,128]{2,1,0:T(8,128)}, u32[]{:S(2)}) %copy-start.3) | copy-done | bytes 16408
  0.8 0.4 %copy-done = f32[53,4,8,128]{3,2,1,0:T(8,128)S(1)} copy-done((f32[53,4,8,128]{3,2,1,0:T(8,128)S(1)}, f32[53,4,8,128]{3,2,1,0:T(8,128)}, u32[]{:S(2)}) %copy-start) | copy-done | bytes 868376
  1.2 0.0 copy-start.6
  1.2 0.2 shard_map.76
  1.4 0.7 %collective-permute-start = (f32[5,56,128]{2,1,0:T(8,128)S(1)}, f32[5,56,128]{2,1,0:T(8,128)S(1)}, u32[]{:S(2)}, u32[]{:S(2)}) collective-permute-start(f32[5,56,128]{2,1,0:T(8,128)S(1)} %get-tuple-element.28), channel_id=1, source_target_pairs={{0,1},{1,0},{2,3},{3,2},{4,5},{5,4},{6,7},{7,6},{8,9},{9,8},{10,11... | collective-permute-start | bytes 430088 | tf_op jit(solution)/shard_map/ppermute | solution.py:27
  2.1 0.0 copy-start.1
  2.1 3.1 %collective-permute-start.1 = (f32[5,56,128]{2,1,0:T(8,128)S(1)}, f32[5,56,128]{2,1,0:T(8,128)S(1)}, u32[]{:S(2)}, u32[]{:S(2)}) collective-permute-start(f32[5,56,128]{2,1,0:T(8,128)S(1)} %get-tuple-element.29), channel_id=1, source_target_pairs={{1,2},{2,1},{5,6},{6,5},{9,10},{10,9},{13,14},{14,13},{17,18},{18,... | collective-permute-start | bytes 430088 | tf_op jit(solution)/shard_map/ppermute | solution.py:27
  5.2 1.3 %collective-permute-start.3 = (f32[424,128]{1,0:T(8,128)S(1)}, f32[424,128]{1,0:T(8,128)S(1)}, u32[]{:S(2)}, u32[]{:S(2)}) collective-permute-start(f32[424,128]{1,0:T(8,128)S(1)} %get-tuple-element.33), channel_id=1, source_target_pairs={{0,4},{4,0},{8,12},{12,8},{16,20},{20,16},{24,28},{28,24},{1,5},{5... | collective-permute-start | bytes 651272 | tf_op jit(solution)/shard_map/ppermute | solution.py:27
  6.5 0.0 copy-done.6
  6.5 0.0 copy-done.1
  6.5 0.1 copy_multiply_fusion
  6.6 0.0 copy-start.2
  6.6 0.0 copy-start.4
  6.6 0.0 copy-start.5
  6.6 0.7 %copy-done.2 = f32[53,53]{1,0:T(8,128)S(1)} copy-done((f32[53,53]{1,0:T(8,128)S(1)}, f32[53,53]{1,0:T(8,128)}, u32[]{:S(2)}) %copy-start.2) | copy-done | bytes 11260
  7.3 0.0 copy-done.4
  7.3 0.0 copy-done.5
  7.3 0.6 %shard_map.73 = (f32[56,128]{1,0:T(8,128)S(1)}, f32[4,8,128]{2,1,0:T(8,128)S(1)}, s32[8,128]{1,0:T(8,128)S(1)}, f32[53,53]{1,0:T(8,128)S(1)}) custom-call(f32[4]{0:T(128)S(1)} %copy-done.1, s32[4]{0:T(128)S(1)} %copy-done.4, f32[53]{0:T(128)S(1)} %copy-done.5, f32[53,53]{1,0:T(8,128)S(1)} %copy-done.2), custom_call_target="tpu_custom_call" | custom-call | flops 500000000 | bytes 1 | tf_op jit(solution)/shard_map/pallas_call | solution.py:333
  7.9 0.6 %shard_map.74 = (f32[4,8,56,128]{3,2,1,0:T(8,128)S(1)}, bf16[64,192]{1,0:T(8,128)(2,1)S(1)}, bf16[224,192]{1,0:T(8,128)(2,1)S(1)}) custom-call(f32[1696,128]{1,0:T(8,128)S(1)} %bitcast.2, f32[53,53]{1,0:T(8,128)S(1)} %get-tuple-element.26.mixing, f32[4,53,53]{2,1,0:T(8,128)S(1)} %rev.3.inverses), custom_call_target="tpu_custom_call" | custom-call | flops 1000000000 | bytes 1 | tf_op jit(solution)/shard_map/pallas_call | solution.py:333
  8.5 0.0 collective-permute-done.ya
  8.5 0.3 %collective-permute-done.1.yb = f32[5,56,128]{2,1,0:T(8,128)S(1)} collective-permute-done((f32[5,56,128]{2,1,0:T(8,128)S(1)}, f32[5,56,128]{2,1,0:T(8,128)S(1)}, u32[]{:S(2)}, u32[]{:S(2)}) %collective-permute-start.1) | collective-permute-done | bytes 143392 | tf_op jit(solution)/shard_map/ppermute | solution.py:27
  8.8 0.3 %shard_map.77 = f32[962,128]{1,0:T(8,128)S(1)} custom-call(f32[1696,128]{1,0:T(8,128)S(1)} %bitcast.3, f32[5,56,128]{2,1,0:T(8,128)S(1)} %collective-permute-done.ya, f32[5,56,128]{2,1,0:T(8,128)S(1)} %collective-permute-done.1.yb, f32[4,8,128]{2,1,0:T(8,128)S(1)} %shard_map.75.cls, f32[56,128]{1,0:T(8,128)S(1)} %get-tuple-element.30.scale), custom_call_target="tpu_custom_call" | custom-call | flops 500000000 | bytes 1 | tf_op jit(solution)/shard_map/pallas_call | solution.py:333
  9.1 3.0 %collective-permute-start.2 = (f32[962,128]{1,0:T(8,128)S(1)}, f32[962,128]{1,0:T(8,128)S(1)}, u32[]{:S(2)}, u32[]{:S(2)}) collective-permute-start(f32[962,128]{1,0:T(8,128)S(1)} %shard_map.77), channel_id=1, source_target_pairs={{4,8},{8,4},{12,16},{16,12},{20,24},{24,20},{5,9},{9,5},{13,17},{1... | collective-permute-start | bytes 1477640 | tf_op jit(solution)/shard_map/ppermute | solution.py:27
  12.2 0.0 collective-permute-done.3.halo
  12.2 5.6 %shard_map.78 = (f32[4,8,56,128]{3,2,1,0:T(8,128)S(1)}, f32[4,8,56,128]{3,2,1,0:T(8,128)S(1)}, f32[424,128]{1,0:T(8,128)S(1)}, f32[4,56,128]{2,1,0:T(8,128)S(1)}, f32[4,56,128]{2,1,0:T(8,128)S(1)}) custom-call(f32[4,8,128]{2,1,0:T(8,128)S(1)} %get-tuple-element.24.inverse, s32[8,128]{1,0:T(8,128)S(1)} %get-tuple-element.25.counts, ...), custom_call_target="tpu_custom_call" | custom-call | flops 6000000000 | bytes 1 | tf_op jit(solution)/shard_map/pallas_call | solution.py:333
  17.7 0.1 collective-permute-start.5
  17.8 3.1 %collective-permute-start.6 = (f32[4,56,128]{2,1,0:T(8,128)S(1)}, f32[4,56,128]{2,1,0:T(8,128)S(1)}, u32[]{:S(2)}, u32[]{:S(2)}) collective-permute-start(f32[4,56,128]{2,1,0:T(8,128)S(1)} %get-tuple-element.41), channel_id=1, source_target_pairs={{1,2},{2,1},{5,6},{6,5},{9,10},{10,9},{13,14},{14,13},{17,18},{18,... | collective-permute-start | bytes 344072 | tf_op jit(solution)/shard_map/ppermute | solution.py:27
  20.9 0.1 collective-permute-start.4
  21.0 2.2 %collective-permute-done.2.message = f32[962,128]{1,0:T(8,128)S(1)} collective-permute-done((f32[962,128]{1,0:T(8,128)S(1)}, f32[962,128]{1,0:T(8,128)S(1)}, u32[]{:S(2)}, u32[]{:S(2)}) %collective-permute-start.2) | collective-permute-done | bytes 492576 | tf_op jit(solution)/shard_map/ppermute | solution.py:27
  23.2 4.5 %shard_map.79 = (f32[4,8,56,128]{3,2,1,0:T(8,128)S(1)}, f32[4,8,56,128]{3,2,1,0:T(8,128)S(1)}, f32[8,56,128]{2,1,0:T(8,128)S(1)}, f32[2,56,128]{2,1,0:T(8,128)S(1)}) custom-call(f32[4,8,128]{2,1,0:T(8,128)S(1)} %get-tuple-element.24.inverse, s32[8,128]{1,0:T(8,128)S(1)} %get-tuple-element.25.counts, ...), custom_call_target="tpu_custom_call", output_to_operand_aliasing={{0}: (10, {}), {1}: (11, {})} | custom-call | flops 5000000000 | bytes 1 | tf_op jit(solution)/shard_map/pallas_call | solution.py:333
  27.7 0.0 collective-permute-done.5.ya
  27.7 0.0 collective-permute-done.6.yb
  27.7 0.0 collective-permute-done.4.xa
  27.8 1.4 %shard_map.80 = f32[53,4,8,128]{3,2,1,0:T(8,128)} custom-call(f32[4,8,56,128]{3,2,1,0:T(8,128)S(1)} %get-tuple-element.36.sec, f32[4,8,56,128]{3,2,1,0:T(8,128)S(1)} %get-tuple-element.37.f_ref, f32[424,128]{1,0:T(8,128)S(1)} %collective-permute-done.4.xa, f32[8,56,128]{2,1,0:T(8,128)S(1)} %get-tuple-element.39.beyond, ...), custom_call_target="tpu_custom_call" | custom-call | flops 2000000000 | bytes 1 | tf_op jit(solution)/shard_map/pallas_call | solution.py:333
  (2 shorter events, 0.0 us)
Async XLA Ops:
  0.0 1.2 %copy-start = (f32[53,4,8,128]{3,2,1,0:T(8,128)S(1)}, f32[53,4,8,128]{3,2,1,0:T(8,128)}, u32[]{:S(2)}) copy-start(f32[53,4,8,128]{3,2,1,0:T(8,128)} %param.7) | copy-start | bytes 2605060
  0.0 0.8 %copy-start.3 = (s32[4,8,128]{2,1,0:T(8,128)S(1)}, s32[4,8,128]{2,1,0:T(8,128)}, u32[]{:S(2)}) copy-start(s32[4,8,128]{2,1,0:T(8,128)} %cell_class.1) | copy-start | bytes 49156
  1.2 5.3 %copy-start.6 = (f32[4,53,53]{2,0,1:T(4,128)S(1)}, f32[4,53,53]{2,0,1:T(4,128)}, u32[]{:S(2)}) copy-start(f32[4,53,53]{2,0,1:T(4,128)} %param.11) | copy-start | bytes 134836
  1.4 7.1 %collective-permute-start = (f32[5,56,128]{2,1,0:T(8,128)S(1)}, f32[5,56,128]{2,1,0:T(8,128)S(1)}, u32[]{:S(2)}, u32[]{:S(2)}) collective-permute-start(f32[5,56,128]{2,1,0:T(8,128)S(1)} %get-tuple-element.28), channel_id=1, source_target_pairs={{0,1},{1,0},{2,3},{3,2},{4,5},{5,4},{6,7},{7,6},{8,9},{9,8},{10,11... | collective-permute-start | bytes 430088 | tf_op jit(solution)/shard_map/ppermute | solution.py:27
  2.1 4.3 %copy-start.1 = (f32[4]{0:T(128)S(1)}, f32[4]{0:T(128)}, u32[]{:S(2)}) copy-start(f32[4]{0:T(128)} %rate.1) | copy-start | bytes 52
  2.1 6.7 %collective-permute-start.1 = (f32[5,56,128]{2,1,0:T(8,128)S(1)}, f32[5,56,128]{2,1,0:T(8,128)S(1)}, u32[]{:S(2)}, u32[]{:S(2)}) collective-permute-start(f32[5,56,128]{2,1,0:T(8,128)S(1)} %get-tuple-element.29), channel_id=1, source_target_pairs={{1,2},{2,1},{5,6},{6,5},{9,10},{10,9},{13,14},{14,13},{17,18},{18,... | collective-permute-start | bytes 430088 | tf_op jit(solution)/shard_map/ppermute | solution.py:27
  5.2 7.0 %collective-permute-start.3 = (f32[424,128]{1,0:T(8,128)S(1)}, f32[424,128]{1,0:T(8,128)S(1)}, u32[]{:S(2)}, u32[]{:S(2)}) collective-permute-start(f32[424,128]{1,0:T(8,128)S(1)} %get-tuple-element.33), channel_id=1, source_target_pairs={{0,4},{4,0},{8,12},{12,8},{16,20},{20,16},{24,28},{28,24},{1,5},{5... | collective-permute-start | bytes 651272 | tf_op jit(solution)/shard_map/ppermute | solution.py:27
  6.6 0.7 %copy-start.2 = (f32[53,53]{1,0:T(8,128)S(1)}, f32[53,53]{1,0:T(8,128)}, u32[]{:S(2)}) copy-start(f32[53,53]{1,0:T(8,128)} %mixing.1) | copy-start | bytes 33712
  6.6 0.7 %copy-start.4 = (s32[4]{0:T(128)S(1)}, s32[4]{0:T(128)}, u32[]{:S(2)}) copy-start(s32[4]{0:T(128)} %count.1) | copy-start | bytes 52
  6.6 0.7 %copy-start.5 = (f32[53]{0:T(128)S(1)}, f32[53]{0:T(128)}, u32[]{:S(2)}) copy-start(f32[53]{0:T(128)} %dif.1) | copy-start | bytes 640
  9.1 14.0 %collective-permute-start.2 = (f32[962,128]{1,0:T(8,128)S(1)}, f32[962,128]{1,0:T(8,128)S(1)}, u32[]{:S(2)}, u32[]{:S(2)}) collective-permute-start(f32[962,128]{1,0:T(8,128)S(1)} %shard_map.77), channel_id=1, source_target_pairs={{4,8},{8,4},{12,16},{16,12},{20,24},{24,20},{5,9},{9,5},{13,17},{1... | collective-permute-start | bytes 1477640 | tf_op jit(solution)/shard_map/ppermute | solution.py:27
  17.7 10.0 %collective-permute-start.5 = (f32[4,56,128]{2,1,0:T(8,128)S(1)}, f32[4,56,128]{2,1,0:T(8,128)S(1)}, u32[]{:S(2)}, u32[]{:S(2)}) collective-permute-start(f32[4,56,128]{2,1,0:T(8,128)S(1)} %get-tuple-element.40), channel_id=1, source_target_pairs={{0,1},{1,0},{2,3},{3,2},{4,5},{5,4},{6,7},{7,6},{8,9},{9,8},{10,11... | collective-permute-start | bytes 344072 | tf_op jit(solution)/shard_map/ppermute | solution.py:27
  17.8 9.9 %collective-permute-start.6 = (f32[4,56,128]{2,1,0:T(8,128)S(1)}, f32[4,56,128]{2,1,0:T(8,128)S(1)}, u32[]{:S(2)}, u32[]{:S(2)}) collective-permute-start(f32[4,56,128]{2,1,0:T(8,128)S(1)} %get-tuple-element.41), channel_id=1, source_target_pairs={{1,2},{2,1},{5,6},{6,5},{9,10},{10,9},{13,14},{14,13},{17,18},{18,... | collective-permute-start | bytes 344072 | tf_op jit(solution)/shard_map/ppermute | solution.py:27
  20.9 6.9 %collective-permute-start.4 = (f32[424,128]{1,0:T(8,128)S(1)}, f32[424,128]{1,0:T(8,128)S(1)}, u32[]{:S(2)}, u32[]{:S(2)}) collective-permute-start(f32[424,128]{1,0:T(8,128)S(1)} %get-tuple-element.38), channel_id=1, source_target_pairs={{0,4},{4,0},{8,12},{12,8},{16,20},{20,16},{24,28},{28,24},{1,5},{5... | collective-permute-start | bytes 651272 | tf_op jit(solution)/shard_map/ppermute | solution.py:27
